TPU v7x, 128 devices: a whole 4x4x4 slice. The times are simulated.
128 devices in a mesh: dp: 16 (over z, y), sp: 8 (over x, core).
Axes of the slice: x: 4, y: 4, z: 4, core: 2. Of those that a mesh axis runs over, the one named last changes fastest.
Arguments:
- tokens: bfloat16 [16, 2048, 2048], P('dp', 'sp')
- grad_out: bfloat16 [16, 2048, 2048], P('dp', 'sp')
- norm_attn: bfloat16 [2048], replicated
- w_query: bfloat16 [2048, 2048], replicated
- w_key: bfloat16 [2048, 1024], replicated
- w_value: bfloat16 [2048, 1024], replicated
- w_out: bfloat16 [2048, 2048], replicated
- norm_mlp: bfloat16 [2048], replicated
- w_gate: bfloat16 [2048, 6144], replicated
- w_up: bfloat16 [2048, 6144], replicated
- w_down: bfloat16 [6144, 2048], replicated
Outputs:
- output 1: bfloat16 [16, 2048, 2048], P('dp', 'sp')
- output 2: float32 [2048], replicated
- output 3: float32 [2048, 2048], replicated
- output 4: float32 [2048, 1024], replicated
- output 5: float32 [2048, 1024], replicated
- output 6: float32 [2048, 2048], replicated
- output 7: float32 [2048], replicated
- output 8: float32 [2048, 6144], replicated
- output 9: float32 [2048, 6144], replicated
- output 10: float32 [6144, 2048], replicated
All inputs are finite; a program needn't handle non-finite values.
Results may differ from a plain program's by a relative error of at most 0.02.
Values are sent between devices in bfloat16 or wider.
A program may use at most 1.25 GiB of HBM per device.

v0:
```python
import functools
import math

import jax
import jax.numpy as jnp
from jax import lax
from jax.experimental import pallas as pl
from jax.experimental.pallas import tpu as pltpu
from jax.sharding import PartitionSpec as P


NORM_EPS = 1.0e-5
ROPE_BASE = 1.0e6
HEAD_DIM = 128
F32 = jnp.float32
BF16 = jnp.bfloat16
VMEM_LIMIT = 60 * 1024 * 1024
MESH = pl.DeviceIdType.MESH
NEG = -1.0e30


def nn(a, b):
    return lax.dot_general(a, b, (((1,), (0,)), ((), ())), preferred_element_type=F32)


def nt(a, b):
    return lax.dot_general(a, b, (((1,), (1,)), ((), ())), preferred_element_type=F32)


def tn(a, b):
    return lax.dot_general(a, b, (((0,), (0,)), ((), ())), preferred_element_type=F32)


def norm_fwd(values, gain_vec):
    values_f = values.astype(F32)
    inv_rms = lax.rsqrt(jnp.mean(values_f * values_f, axis=-1, keepdims=True) + NORM_EPS)
    unit_vals = values_f * inv_rms
    return (unit_vals * gain_vec.astype(F32)).astype(BF16), unit_vals, inv_rms


def norm_bwd(grad_normed, unit_vals, inv_rms, gain_vec):
    grad_f = grad_normed.astype(F32)
    grad_gain = jnp.sum(grad_f * unit_vals, axis=0)
    grad_unit = grad_f * gain_vec.astype(F32)
    grad_in = inv_rms * (grad_unit - unit_vals * jnp.mean(grad_unit * unit_vals, axis=-1, keepdims=True))
    return grad_in, grad_gain


def rope_tables(positions):
    half_dim = HEAD_DIM // 2
    inv_freq = ROPE_BASE ** (-jnp.arange(half_dim, dtype=F32) * (2.0 / HEAD_DIM))
    angles = positions.astype(F32)[:, None] * inv_freq[None, :]
    cos, sin = jnp.cos(angles), jnp.sin(angles)
    return jnp.concatenate([cos, cos], axis=-1), jnp.concatenate([-sin, sin], axis=-1)


def rope(values, cos_tab, sin_tab):
    return values * cos_tab + pltpu.roll(values, HEAD_DIM // 2, 1) * sin_tab


def call(kernel, flops, moved, **kwargs):
    params = pltpu.CompilerParams(vmem_limit_bytes=VMEM_LIMIT)
    cost = pl.CostEstimate(flops=int(flops), bytes_accessed=int(moved), transcendentals=0)
    return pl.pallas_call(kernel, compiler_params=params, cost_estimate=cost, **kwargs)


def whole(shape):
    return pl.BlockSpec(shape, lambda *_: (0,) * len(shape))


def gather_qkv_kernel(x_ref, wq_ref, wk_ref, wv_ref, cos_blk, sin_blk, cos_row, sin_row, full_ref, qkv_ref, land, weights, w_sems, o_sems, i_send, i_recv, d_send, d_recv):
    x, c = lax.axis_index("x"), lax.axis_index("c")
    n = land.shape[0] // 2
    tok = x_ref.shape[0]
    half = tok // 2
    qw, kw = wq_ref.shape[1] // (2 * n), wk_ref.shape[1] // (2 * n)
    width = qw + 2 * kw
    wrap = lambda v: lax.rem(v + 2 * n, n)
    at = lambda dx, core: 2 * wrap(x + dx) + core
    me = 2 * x + c

    loads = []
    for k, (ref, start, size) in enumerate(((wq_ref, 0, qw), (wk_ref, qw, kw), (wv_ref, qw + kw, kw))):
        cols = pl.ds(pl.multiple_of(me * size, 128), size)
        loads.append(pltpu.make_async_copy(ref.at[:, cols], weights.at[:, pl.ds(start, size)], w_sems.at[k]))
        loads[-1].start()

    barrier = pltpu.get_barrier_semaphore()
    for goal in ({"x": wrap(x + 1)}, {"x": wrap(x - 1)}, {"c": 1 - c}):
        pl.semaphore_signal(barrier, inc=1, device_id=goal, device_id_type=MESH)
    pl.semaphore_wait(barrier, 3)

    rows = lambda h: pl.ds(h * half, half)

    def ring(way, hop, h):
        k = (0 if way > 0 else 3) + (h if hop == 0 else 2)
        src = land.at[at(-way * hop, c), rows(h)] if hop else x_ref.at[rows(h)]
        dst = land.at[at(-way * hop, c), rows(h)]
        return pltpu.make_async_remote_copy(src, dst, i_send.at[k], i_recv.at[k], device_id={"x": wrap(x + way)}, device_id_type=MESH)

    def across(k, dx, h):
        part = rows(h) if h is not None else pl.ds(0, tok)
        src = land.at[at(dx, c), part] if dx else x_ref.at[part]
        return pltpu.make_async_remote_copy(src, land.at[at(dx, c), part], d_send.at[k], d_recv.at[k], device_id={"c": 1 - c}, device_id_type=MESH)

    first = [ring(1, 0, 0), ring(-1, 0, 1), ring(1, 0, 1), ring(-1, 0, 0)]
    second = [ring(1, 1, 0), ring(-1, 1, 1)]
    die = [across(0, 0, None), across(1, -1, 0), across(2, 1, 1), across(3, -1, 1), across(4, 1, 0), across(5, 2, 0), across(6, 2, 1)]
    for copy in first[:2] + die[:1] + first[2:]:
        copy.start()
    land[me] = x_ref[...]
    for load in loads:
        load.wait()

    def wait_block(k):
        @pl.when(k == 1)
        def _():
            die[0].wait_recv()

        @pl.when(k == 2)
        def _():
            first[0].wait_recv()
            second[0].start()
            die[1].start()
            first[1].wait_recv()
            second[1].start()
            die[2].start()
            first[2].wait_recv()
            die[3].start()

        @pl.when(k == 3)
        def _():
            first[3].wait_recv()
            die[4].start()

        @pl.when(k == 4)
        def _():
            die[1].wait_recv()
            die[3].wait_recv()

        @pl.when(k == 5)
        def _():
            die[2].wait_recv()
            die[4].wait_recv()

        @pl.when(k == 6)
        def _():
            second[0].wait_recv()
            die[5].start()
            second[1].wait_recv()
            die[6].start()

        @pl.when(k == 7)
        def _():
            die[5].wait_recv()
            die[6].wait_recv()

    def out_copy(k):
        dx = jnp.where(k < 2, 0, jnp.where(k >= 6, 2, jnp.where(lax.rem(k, 2) == 0, -1, 1)))
        core = jnp.where((k == 1) | (k == 4) | (k == 5) | (k == 7), 1 - c, c)
        block = 2 * wrap(x + dx) + core
        here = pl.ds(pl.multiple_of(block * tok, tok), tok)
        return block, here, pltpu.make_async_copy(land.at[block], full_ref.at[here, :], o_sems.at[k])

    def body(k, carry):
        wait_block(k)
        block, here, copy = out_copy(k)
        copy.start()
        value = nn(land[block], weights[...])
        cos_b, sin_b = cos_blk[pl.ds(block, 1), :], sin_blk[pl.ds(block, 1), :]
        cos = cos_b * cos_row[...] - sin_b * sin_row[...]
        sin = sin_b * cos_row[...] + cos_b * sin_row[...]
        for start in range(0, width, HEAD_DIM):
            part = value[:, start : start + HEAD_DIM]
            if start < qw + kw:
                part = rope(part, cos, sin)
            qkv_ref[here, start : start + HEAD_DIM] = part.astype(BF16)
        return carry

    lax.fori_loop(0, 2 * n, body, 0)
    for copy in first + second + die:
        copy.wait_send()
    for k in range(2 * n):
        out_copy(k)[2].wait()


def gather_qkv(normed, w_query, w_key, w_value, groups, collective_id):
    tok, dim = normed.shape
    width = (w_query.shape[1] + w_key.shape[1] + w_value.shape[1]) // groups
    anywhere = pl.BlockSpec(memory_space=pl.ANY)
    vmem = pl.BlockSpec(memory_space=pltpu.VMEM)
    return pl.pallas_call(
        gather_qkv_kernel,
        in_specs=[vmem, anywhere, anywhere, anywhere, vmem, vmem, vmem, vmem],
        out_specs=[anywhere, vmem],
        out_shape=[jax.ShapeDtypeStruct((groups * tok, dim), BF16), jax.ShapeDtypeStruct((groups * tok, width), BF16)],
        scratch_shapes=[
            pltpu.VMEM((groups, tok, dim), BF16),
            pltpu.VMEM((dim, width), BF16),
            pltpu.SemaphoreType.DMA((3,)),
            pltpu.SemaphoreType.DMA((groups,)),
            pltpu.SemaphoreType.DMA((6,)),
            pltpu.SemaphoreType.DMA((6,)),
            pltpu.SemaphoreType.DMA((7,)),
            pltpu.SemaphoreType.DMA((7,)),
        ],
        compiler_params=pltpu.CompilerParams(collective_id=collective_id, has_side_effects=True, vmem_limit_bytes=VMEM_LIMIT),
        cost_estimate=pl.CostEstimate(flops=20_000_000_000, bytes_accessed=6 * groups * tok * dim, transcendentals=0),
        name="gather_qkv",
    )(normed, w_query, w_key, w_value, *rope_tables(jnp.arange(groups) * tok), *rope_tables(jnp.arange(tok)))


def attn_fwd_kernel(blk, n_q, qkv_ref, out_ref, lse_ref, tok_ref, mine, land, send_sems, recv_sems, *scrs):
    step, steps = pl.program_id(0), pl.num_programs(0)
    x, c = lax.axis_index("x"), lax.axis_index("c")
    me = 2 * x + c
    tok = blk // 2

    def block_of(step):
        ahead = jnp.where(step == 0, 2, jnp.where(step == 1, 1, jnp.where(step == 2, steps - 1, 0)))
        return lax.rem(x + ahead, steps)

    def send(step, core):
        goal = block_of(step)
        src = mine.at[2 * goal + core]
        return pltpu.make_async_remote_copy(src, land.at[me], send_sems.at[step, core], recv_sems.at[me], device_id={"x": goal, "c": core}, device_id_type=MESH)

    @pl.when(step == 0)
    def _():
        barrier = pltpu.get_barrier_semaphore()
        for k in range(1, 2 * steps):
            peer = lax.rem(me + k, 2 * steps)
            pl.semaphore_signal(barrier, inc=1, device_id={"x": peer // 2, "c": lax.rem(peer, 2)}, device_id_type=MESH)
        pl.semaphore_wait(barrier, 2 * steps - 1)

    @pl.when(step > 0)
    def _():
        send(step - 1, 0).start()
        send(step - 1, 1).start()

    i = block_of(step)
    coef = HEAD_DIM**-0.5 * math.log2(math.e)
    k_at, v_at = n_q * HEAD_DIM, (n_q + 1) * HEAD_DIM
    at = lambda j: pl.ds(pl.multiple_of(j * blk, blk), blk)
    lanes = lambda t, op: functools.reduce(op, [t[:, s : s + 128] for s in range(0, blk, 128)])
    qs = [qkv_ref[at(i), h * HEAD_DIM : (h + 1) * HEAD_DIM] for h in range(n_q)]
    causal = lax.broadcasted_iota(jnp.int32, (blk, blk), 0) >= lax.broadcasted_iota(jnp.int32, (blk, blk), 1)

    def score_step(j, tops, masked):
        key = qkv_ref[at(j), k_at:v_at]
        new = []
        for h in range(n_q):
            s = nt(qs[h], key)
            if masked:
                s = jnp.where(causal, s, NEG)
            scrs[h][:, at(j)] = s
            new.append(jnp.maximum(tops[h], lanes(s, jnp.maximum)))
        return tuple(new)

    start = tuple(jnp.full((blk, 128), NEG, F32) for _ in range(n_q))
    tops = lax.fori_loop(0, i, lambda j, t: score_step(j, t, False), start)
    tops = score_step(i, tops, True)
    row_max = [jnp.max(t, axis=1, keepdims=True) for t in tops]

    def exp_step(j, sums):
        new = []
        for h in range(n_q):
            e = jnp.exp2((scrs[h][:, at(j)] - row_max[h]) * coef)
            scrs[h][:, at(j)] = e
            new.append(sums[h] + lanes(e, jnp.add))
        return tuple(new)

    sums = lax.fori_loop(0, i + 1, exp_step, tuple(jnp.zeros((blk, 128), F32) for _ in range(n_q)))
    row_sum = [jnp.sum(t, axis=1, keepdims=True) for t in sums]
    inv_sum = [1.0 / t for t in row_sum]

    def out_step(j, accs):
        value = qkv_ref[at(j), v_at : v_at + HEAD_DIM]
        return tuple(accs[h] + nn((scrs[h][:, at(j)] * inv_sum[h]).astype(BF16), value) for h in range(n_q))

    accs = lax.fori_loop(0, i + 1, out_step, tuple(jnp.zeros((blk, HEAD_DIM), F32) for _ in range(n_q)))
    for h in range(n_q):
        value = accs[h].astype(BF16)
        out_ref[at(i), h * HEAD_DIM : (h + 1) * HEAD_DIM] = value
        for core in range(2):
            mine[2 * i + core, :, h * HEAD_DIM : (h + 1) * HEAD_DIM] = value[core * tok : (core + 1) * tok, :]
        log_norm = row_max[h] * coef + jnp.log2(row_sum[h])
        lse_ref[h * 8 : (h + 1) * 8, at(i)] = jnp.transpose(jnp.broadcast_to(log_norm, (blk, 128)))[:8, :]

    @pl.when(step == steps - 1)
    def _():
        land[me] = mine[me]
        send(step, 1 - c).start()
        for k in range(1, 2 * steps):
            peer = lax.rem(me + k, 2 * steps)
            pltpu.make_async_remote_copy(mine.at[peer], land.at[peer], send_sems.at[0, 0], recv_sems.at[peer], device_id={"x": x, "c": c}, device_id_type=MESH).wait_recv()
        tok_ref[...] = land[...]
        for k in range(steps - 1):
            send(k, 0).wait_send()
            send(k, 1).wait_send()
        send(step, 1 - c).wait_send()


def attn_fwd(qkv, steps, collective_id):
    seq, width = qkv.shape
    n_q = width // HEAD_DIM - 2
    blk = seq // steps
    return pl.pallas_call(
        functools.partial(attn_fwd_kernel, blk, n_q),
        grid=(steps,),
        in_specs=[whole((seq, width))],
        out_specs=[whole((seq, n_q * HEAD_DIM)), whole((8 * n_q, seq)), whole((2 * steps, blk // 2, n_q * HEAD_DIM))],
        out_shape=[
            jax.ShapeDtypeStruct((seq, n_q * HEAD_DIM), BF16),
            jax.ShapeDtypeStruct((8 * n_q, seq), F32),
            jax.ShapeDtypeStruct((2 * steps, blk // 2, n_q * HEAD_DIM), BF16),
        ],
        scratch_shapes=[pltpu.VMEM((2 * steps, blk // 2, n_q * HEAD_DIM), BF16)] * 2
        + [pltpu.SemaphoreType.DMA((steps, 2)), pltpu.SemaphoreType.DMA((2 * steps,))]
        + [pltpu.VMEM((blk, seq), F32)] * n_q,
        compiler_params=pltpu.CompilerParams(collective_id=collective_id, has_side_effects=True, vmem_limit_bytes=VMEM_LIMIT),
        cost_estimate=pl.CostEstimate(flops=2 * n_q * seq * seq * HEAD_DIM * 2, bytes_accessed=seq * width * 2, transcendentals=0),
        name="attn_fwd",
    )(qkv)


def attn_bwd_kernel(blk, n_q, qkv_ref, do_ref, lse_ref, cos_ref, sin_ref, out_ref, dk_scr, dv_scr, *scrs):
    i, steps = pl.program_id(0), pl.num_programs(0)
    scale = HEAD_DIM**-0.5
    coef = scale * math.log2(math.e)
    k_at, v_at = n_q * HEAD_DIM, (n_q + 1) * HEAD_DIM
    at = lambda j: pl.ds(pl.multiple_of(j * blk, blk), blk)
    p_scrs, dp_scrs = scrs[:n_q], scrs[n_q:]
    qs = [qkv_ref[at(i), h * HEAD_DIM : (h + 1) * HEAD_DIM] for h in range(n_q)]
    dos = [do_ref[:, h * HEAD_DIM : (h + 1) * HEAD_DIM] for h in range(n_q)]
    lses = [lse_ref[h * 8 : h * 8 + 1, :] for h in range(n_q)]
    causal = lax.broadcasted_iota(jnp.int32, (blk, blk), 0) <= lax.broadcasted_iota(jnp.int32, (blk, blk), 1)

    @pl.when(i == 0)
    def _():
        dk_scr[...] = jnp.zeros_like(dk_scr)
        dv_scr[...] = jnp.zeros_like(dv_scr)

    def prob_step(j, dots, masked):
        key, value = qkv_ref[at(j), k_at:v_at], qkv_ref[at(j), v_at : v_at + HEAD_DIM]
        new, dv = [], dv_scr[at(j), :]
        for h in range(n_q):
            p = jnp.exp2(nt(key, qs[h]) * coef - lses[h])
            if masked:
                p = jnp.where(causal, p, 0.0)
            dp = nt(value, dos[h]).astype(BF16)
            p_scrs[h][at(j), :] = p
            dp_scrs[h][at(j), :] = dp
            dv = dv + nn(p.astype(BF16), dos[h])
            new.append(dots[h] + jnp.sum((p * dp.astype(F32)).reshape(blk // 8, 8, blk), axis=0))
        dv_scr[at(j), :] = dv
        return tuple(new)

    dots = lax.fori_loop(0, i, lambda j, t: prob_step(j, t, False), tuple(jnp.zeros((8, blk), F32) for _ in range(n_q)))
    dots = prob_step(i, dots, True)
    row_dot = [jnp.sum(t, axis=0, keepdims=True) for t in dots]

    def grad_step(j, accs):
        key = qkv_ref[at(j), k_at:v_at]
        new, dk = [], dk_scr[at(j), :]
        for h in range(n_q):
            ds = (p_scrs[h][at(j), :] * (dp_scrs[h][at(j), :].astype(F32) - row_dot[h]) * scale).astype(BF16)
            dk = dk + nn(ds, qs[h])
            new.append(accs[h] + tn(ds, key))
        dk_scr[at(j), :] = dk
        return tuple(new)

    accs = lax.fori_loop(0, i + 1, grad_step, tuple(jnp.zeros((blk, HEAD_DIM), F32) for _ in range(n_q)))
    unrope = lambda g, sl: rope(g.astype(BF16).astype(F32), cos_ref[sl, :], -sin_ref[sl, :]).astype(BF16)
    for h in range(n_q):
        out_ref[at(i), h * HEAD_DIM : (h + 1) * HEAD_DIM] = unrope(accs[h], at(i))

    @pl.when(i == steps - 1)
    def _():
        def finish(j, carry):
            out_ref[at(j), k_at:v_at] = unrope(dk_scr[at(j), :], at(j))
            out_ref[at(j), v_at : v_at + HEAD_DIM] = dv_scr[at(j), :].astype(BF16)
            return carry

        lax.fori_loop(0, steps, finish, 0)


def attn_bwd(qkv, grad_out, lse, cos, sin, blk):
    seq, width = qkv.shape
    n_q = width // HEAD_DIM - 2
    return call(
        functools.partial(attn_bwd_kernel, blk, n_q),
        5 * n_q * seq * seq * HEAD_DIM * 2,
        seq * width * 4,
        grid=(seq // blk,),
        in_specs=[
            whole((seq, width)),
            pl.BlockSpec((blk, n_q * HEAD_DIM), lambda i: (i, 0)),
            pl.BlockSpec((8 * n_q, blk), lambda i: (0, i)),
            whole((seq, HEAD_DIM)),
            whole((seq, HEAD_DIM)),
        ],
        out_specs=whole((seq, width)),
        out_shape=jax.ShapeDtypeStruct((seq, width), BF16),
        scratch_shapes=[pltpu.VMEM((seq, HEAD_DIM), F32)] * 2
        + [pltpu.VMEM((seq, blk), F32)] * n_q
        + [pltpu.VMEM((seq, blk), BF16)] * n_q,
        name="attn_bwd",
    )(qkv, grad_out, lse, cos, sin)


def act_grads(gate, up, grad_act):
    sig = 1.0 / (1.0 + jnp.exp(-gate))
    act = gate * sig
    grad_gate = (grad_act * up * sig * (1.0 + gate * (1.0 - sig))).astype(BF16)
    grad_up = (grad_act * act).astype(BF16)
    return (act * up).astype(BF16), grad_gate, grad_up


def mlp_kernel(m_ref, dy_ref, wg_ref, wu_ref, wd_ref, out_ref, acc_ref):
    step = pl.program_id(0)
    m, dy = m_ref[...], dy_ref[...]
    grad_act = nt(dy, wd_ref[...]).astype(BF16).astype(F32)
    _, grad_gate, grad_up = act_grads(nn(m, wg_ref[...]), nn(m, wu_ref[...]), grad_act)
    total = nt(grad_gate, wg_ref[...]) + nt(grad_up, wu_ref[...])

    @pl.when(step == 0)
    def _():
        acc_ref[...] = total

    @pl.when(step > 0)
    def _():
        acc_ref[...] += total

    @pl.when(step == pl.num_programs(0) - 1)
    def _():
        out_ref[...] = acc_ref[...].astype(BF16)


def mlp_grad_input(m, dy, w_gate, w_up, w_down, blk):
    tok, dim = m.shape
    width = w_gate.shape[1]
    return call(
        mlp_kernel,
        5 * 2 * tok * dim * width,
        3 * 2 * dim * width,
        grid=(width // blk,),
        in_specs=[
            whole((tok, dim)),
            whole((tok, dim)),
            pl.BlockSpec((dim, blk), lambda j: (0, j)),
            pl.BlockSpec((dim, blk), lambda j: (0, j)),
            pl.BlockSpec((blk, dim), lambda j: (j, 0)),
        ],
        out_specs=whole((tok, dim)),
        out_shape=jax.ShapeDtypeStruct((tok, dim), BF16),
        scratch_shapes=[pltpu.VMEM((tok, dim), F32)],
        name="mlp_grad_input",
    )(m, dy, w_gate, w_up, w_down)


class Ring:
    def __init__(self, n, subs, slow, fast, source, recv1, acc, send2, recv2, s1, r1, s2, r2):
        self.n, self.subs, self.slow, self.fast, self.source = n, subs, slow, fast, source
        self.recv1, self.acc, self.send2, self.recv2 = recv1, acc, send2, recv2
        self.s1, self.r1, self.s2, self.r2 = s1, r1, s2, r2
        self.z, self.y = lax.axis_index(slow), lax.axis_index(fast)
        self.height = recv1.shape[5]

    def wrap(self, v):
        return lax.rem(v + 2 * self.n, self.n)

    def goal(self, c, phase):
        step = 1 - 2 * (c % 2)
        if (c < 2) == (phase == 1):
            return {self.fast: self.wrap(self.y + step)}
        return {self.slow: self.wrap(self.z + step)}

    def arrive(self):
        barrier = pltpu.get_barrier_semaphore()
        for c in range(4):
            pl.semaphore_signal(barrier, inc=1, device_id=self.goal(c, 1), device_id_type=MESH)

    def meet(self):
        pl.semaphore_wait(pltpu.get_barrier_semaphore(), 4)

    def coord(self, c, phase):
        return self.y if (c < 2) == (phase == 1) else self.z

    def rows(self, c, s):
        return pl.ds((c * self.subs + s) * self.height, self.height)

    def local(self, b, c, a, s):
        source = self.source(b)
        return source.at[:, a, self.rows(c, s), :] if c < 2 else source.at[a, :, self.rows(c, s), :]

    def chunk(self, c, phase, t):
        return self.wrap(self.coord(c, phase) - (1 - 2 * (c % 2)) * t)

    def copy1(self, b, c, t, s):
        src = self.recv1.at[b, c, t - 1, s] if t else self.local(b, c, self.chunk(c, 1, 1), s)
        dst = self.recv1.at[b, c, t, s]
        return pltpu.make_async_remote_copy(src, dst, self.s1.at[b, c, t, s], self.r1.at[b, c, t, s], device_id=self.goal(c, 1), device_id_type=MESH)

    def copy2(self, b, c, t, s):
        src = self.recv2.at[b, c, t - 1, s] if t else self.send2.at[b, c, s]
        dst = self.recv2.at[b, c, t, s]
        return pltpu.make_async_remote_copy(src, dst, self.s2.at[b, c, t, s], self.r2.at[b, c, t, s], device_id=self.goal(c, 2), device_id_type=MESH)

    def start(self, b):
        for s in range(self.subs):
            for c in range(4):
                self.copy1(b, c, 0, s).start()

    def hop1(self, b, t):
        for s in range(self.subs):
            for c in range(4):
                self.copy1(b, c, t, s).wait_recv()
                mine = self.local(b, c, self.chunk(c, 1, t + 2), s)[...]
                total = self.recv1[b, c, t, s].astype(F32) + mine.astype(F32)
                if t < self.n - 2:
                    self.recv1[b, c, t, s] = total.astype(BF16)
                    self.copy1(b, c, t + 1, s).start()
                else:
                    self.acc[b, c, s] = total
                    self.send2[b, c, s] = self.acc[b, c, s, self.chunk(c, 2, 1)].astype(BF16)
                    self.copy2(b, c, 0, s).start()

    def hop2(self, b, t, scale, store):
        for s in range(self.subs):
            for c in range(4):
                self.copy2(b, c, t, s).wait_recv()
                total = self.recv2[b, c, t, s].astype(F32) + self.acc[b, c, s, self.chunk(c, 2, t + 2)]
                if t < self.n - 2:
                    self.recv2[b, c, t, s] = total.astype(BF16)
                    self.copy2(b, c, t + 1, s).start()
                else:
                    store(b, (c * self.subs + s) * self.height, self.height, (total * scale).astype(BF16))

    def drain(self, b):
        for s in range(self.subs):
            for c in range(4):
                for t in range(self.n - 1):
                    self.copy1(b, c, t, s).wait_send()
                    self.copy2(b, c, t, s).wait_send()

    @staticmethod
    def scratch(n, blocks, subs, rows, width):
        height = rows // (4 * subs)
        return [
            pltpu.VMEM((blocks, 4, n - 1, subs, n, height, width), BF16),
            pltpu.VMEM((blocks, 4, subs, n, height, width), F32),
            pltpu.VMEM((blocks, 4, subs, height, width), BF16),
            pltpu.VMEM((blocks, 4, n - 1, subs, height, width), BF16),
        ] + [pltpu.SemaphoreType.DMA((blocks, 4, n - 1, subs))] * 4


def mlp_ring_kernel(n, subs, scale, blocks, slow, fast, group, m_ref, dy_ref, wg_all, wu_all, wd_all, out_ref, wg_buf, wu_buf, wd_buf, w_sems, grads_ref, act_ref, g_ref, *scratch):
    step = pl.program_id(0)
    seq, dim = m_ref.shape
    width = act_ref.shape[0]
    rows = dim // (n * n)
    tiles = 4
    blk, tile = seq // tiles, dim // tiles
    per_tile = tile // rows
    ring = Ring(n, subs, slow, fast, lambda b: g_ref.at[b], *scratch)
    at = lambda i, size: pl.ds(pl.multiple_of(i * size, size), size)

    def loads(b):
        mine = at((lax.axis_index(group) if group else 0) * blocks + b, width)
        slot = lax.rem(b, 2)
        return [
            pltpu.make_async_copy(wg_all.at[:, mine], wg_buf.at[slot], w_sems.at[slot, 0]),
            pltpu.make_async_copy(wu_all.at[:, mine], wu_buf.at[slot], w_sems.at[slot, 1]),
            pltpu.make_async_copy(wd_all.at[mine, :], wd_buf.at[slot], w_sems.at[slot, 2]),
        ]

    @pl.when(step == 0)
    def _():
        for load in loads(0):
            load.start()
        ring.arrive()
        ring.meet()

    @pl.when(step + 1 < blocks)
    def _():
        for load in loads(step + 1):
            load.start()

    for load in loads(step):
        load.wait()
    wg_ref, wu_ref, wd_ref = (buf.at[lax.rem(step, 2)] for buf in (wg_buf, wu_buf, wd_buf))

    def store(b, first, height, value):
        out_ref[pl.ds(pl.multiple_of(b * 3 * width + first, height), height), :] = value

    hops = [functools.partial(ring.hop1, t=t) for t in range(n - 1)]
    hops += [functools.partial(ring.hop2, t=t, scale=scale, store=store) for t in range(n - 1)]
    slots = 2 * tiles
    delays = [3 * t + 4 if t < n - 1 else 3 * n + 2 * (t - n + 1) for t in range(2 * (n - 1))]

    def events(slot):
        for hop, delay in zip(hops, delays):
            since = slot - delay
            block = since // slots - 1

            @pl.when((since >= slots) & (lax.rem(since, slots) == 0) & (block < blocks))
            def _(hop=hop, block=block):
                hop(block)

    def forward(i):
        m, dy = m_ref[at(i, blk), :], dy_ref[at(i, blk), :]
        grad_act = nt(dy, wd_ref[...]).astype(BF16).astype(F32)
        act, grad_gate, grad_up = act_grads(nn(m, wg_ref[...]), nn(m, wu_ref[...]), grad_act)
        act_ref[:, at(i, blk)] = jnp.transpose(act)
        grads_ref[:width, at(i, blk)] = jnp.transpose(grad_gate)
        grads_ref[width:, at(i, blk)] = jnp.transpose(grad_up)

    def weights(i):
        grads = nn(grads_ref[...], m_ref[:, at(i, tile)]).astype(BF16)
        down = nn(act_ref[...], dy_ref[:, at(i, tile)]).astype(BF16)
        for k in range(per_tile):
            piece = i * per_tile + k
            g_ref[step, piece // n, lax.rem(piece, n), : 2 * width, :] = grads[:, k * rows : (k + 1) * rows]
            g_ref[step, piece // n, lax.rem(piece, n), 2 * width :, :] = down[:, k * rows : (k + 1) * rows]

    def slot_body(i, carry):
        @pl.when(i < tiles)
        def _():
            forward(i)

        @pl.when(i >= tiles)
        def _():
            weights(i - tiles)

        events(step * slots + i)
        return carry

    lax.fori_loop(0, slots, slot_body, 0)
    ring.start(step)

    @pl.when(step == blocks - 1)
    def _():
        def tail(slot, carry):
            events(slot)
            return carry

        lax.fori_loop(blocks * slots, (blocks + 1) * slots + max(delays), tail, 0)

        def drain(b, carry):
            ring.drain(b)
            return carry

        lax.fori_loop(0, blocks, drain, 0)


def mlp_ring(m, dy, w_gate, w_up, w_down, ff, scale, slow, fast, n, group, collective_id):
    seq, dim = m.shape
    width = min(256, ff)
    blocks = ff // width
    subs = 2
    rows = dim // (n * n)
    once = lambda shape: pl.BlockSpec(shape, lambda j: (0, 0), pipeline_mode=pl.Buffered(1))
    anywhere = pl.BlockSpec(memory_space=pl.ANY)
    return pl.pallas_call(
        functools.partial(mlp_ring_kernel, n, subs, scale, blocks, slow, fast, group),
        grid=(blocks,),
        in_specs=[once((seq, dim)), once((seq, dim)), anywhere, anywhere, anywhere],
        out_specs=pl.BlockSpec((3 * ff, rows), lambda j: (0, 0)),
        scratch_shapes=[
            pltpu.VMEM((2, dim, width), BF16),
            pltpu.VMEM((2, dim, width), BF16),
            pltpu.VMEM((2, width, dim), BF16),
            pltpu.SemaphoreType.DMA((2, 3)),
            pltpu.VMEM((2 * width, seq), BF16),
            pltpu.VMEM((width, seq), BF16),
            pltpu.VMEM((blocks, n, n, 3 * width, rows), BF16),
        ]
        + Ring.scratch(n, blocks, subs, 3 * width, rows),
        out_shape=jax.ShapeDtypeStruct((3 * ff, rows), BF16),
        compiler_params=pltpu.CompilerParams(collective_id=collective_id, has_side_effects=True, vmem_limit_bytes=VMEM_LIMIT),
        cost_estimate=pl.CostEstimate(flops=18 * seq * dim * ff, bytes_accessed=4 * seq * dim, transcendentals=0),
        name="mlp_ring",
    )(m, dy, w_gate, w_up, w_down)


def ring_reduce_kernel(n, subs, scale, slow, fast, g_ref, out_ref, *scratch):
    ring = Ring(n, subs, slow, fast, lambda b: g_ref, *scratch)

    def store(b, first, height, value):
        out_ref[first : first + height, :] = value

    ring.arrive()
    ring.meet()
    ring.start(0)
    for t in range(n - 1):
        ring.hop1(0, t)
    for t in range(n - 1):
        ring.hop2(0, t, scale, store)
    ring.drain(0)


def ring_reduce(pieces, scale, subs, slow, fast, collective_id):
    total, rows, width = pieces.shape
    n = round(total**0.5)
    return pl.pallas_call(
        functools.partial(ring_reduce_kernel, n, subs, scale, slow, fast),
        out_shape=jax.ShapeDtypeStruct((rows, width), BF16),
        in_specs=[pl.BlockSpec(memory_space=pltpu.VMEM)],
        out_specs=pl.BlockSpec(memory_space=pltpu.VMEM),
        scratch_shapes=Ring.scratch(n, 1, subs, rows, width),
        compiler_params=pltpu.CompilerParams(collective_id=collective_id, has_side_effects=True, vmem_limit_bytes=VMEM_LIMIT),
        cost_estimate=pl.CostEstimate(flops=40_000_000_000, bytes_accessed=2 * total * rows * width, transcendentals=0),
        name="ring_reduce",
    )(pieces.reshape(n, n, rows, width))


def spread_mlp_kernel(groups, ff_local, width, in_ref, gate_ref, up_ref, down_ref):
    for g in range(groups):
        for at in range(g * ff_local, (g + 1) * ff_local, width):
            gate_ref[:, at : at + width] = jnp.transpose(in_ref[3 * at : 3 * at + width, :]).astype(F32)
            up_ref[:, at : at + width] = jnp.transpose(in_ref[3 * at + width : 3 * at + 2 * width, :]).astype(F32)
            down_ref[at : at + width, :] = in_ref[3 * at + 2 * width : 3 * at + 3 * width, :].astype(F32)


def spread_mlp(stacked, outer, groups, ff_local):
    total, rows = stacked.shape
    ff, dim = ff_local * groups, rows * outer
    return call(
        functools.partial(spread_mlp_kernel, groups, ff_local, min(256, ff_local)),
        total * rows,
        total * rows * 6,
        grid=(outer,),
        in_specs=[pl.BlockSpec((total // outer, rows), lambda o: (o, 0))],
        out_specs=[
            pl.BlockSpec((rows, ff), lambda o: (o, 0)),
            pl.BlockSpec((rows, ff), lambda o: (o, 0)),
            pl.BlockSpec((ff, rows), lambda o: (0, o)),
        ],
        out_shape=[jax.ShapeDtypeStruct((dim, ff), F32)] * 2 + [jax.ShapeDtypeStruct((ff, dim), F32)],
        name="spread_mlp",
    )(stacked)


def spread_attn_kernel(groups, q_width, k_width, in_ref, q_ref, k_ref, v_ref, o_ref, gain_ref):
    rows = q_ref.shape[0]
    gain = None
    for g in range(groups):
        piece = in_ref[g * rows : (g + 1) * rows, :].astype(F32)
        q_ref[:, g * q_width : (g + 1) * q_width] = piece[:, :q_width]
        k_ref[:, g * k_width : (g + 1) * k_width] = piece[:, q_width : q_width + k_width]
        v_ref[:, g * k_width : (g + 1) * k_width] = piece[:, q_width + k_width : q_width + 2 * k_width]
        gain_at, o_at = q_width + 2 * k_width, q_width + 2 * k_width + rows
        block, core = g // 2, g % 2
        o_ref[core * q_width : (core + 1) * q_width, block * rows : (block + 1) * rows] = jnp.transpose(piece[:, o_at:])
        part = piece[:8, gain_at:o_at]
        gain = part if gain is None else gain + part
    gain_ref[...] = gain


def spread_attn(stacked, nz, ny, groups, q_width, k_width):
    total, row_width = stacked.shape
    outer = nz * ny
    rows = total // (outer * groups)
    dim = rows * outer
    nx = groups // 2
    return call(
        functools.partial(spread_attn_kernel, groups, q_width, k_width),
        total * row_width,
        total * row_width * 6,
        grid=(outer,),
        in_specs=[pl.BlockSpec((groups * rows, row_width), lambda o: (o, 0))],
        out_specs=[
            pl.BlockSpec((rows, groups * q_width), lambda o: (o, 0)),
            pl.BlockSpec((rows, groups * k_width), lambda o: (o, 0)),
            pl.BlockSpec((rows, groups * k_width), lambda o: (o, 0)),
            pl.BlockSpec((2 * q_width, nx * rows), lambda o: (o % ny, o // ny)),
            pl.BlockSpec((8, rows), lambda o: (o, 0)),
        ],
        out_shape=[
            jax.ShapeDtypeStruct((dim, groups * q_width), F32),
            jax.ShapeDtypeStruct((dim, groups * k_width), F32),
            jax.ShapeDtypeStruct((dim, groups * k_width), F32),
            jax.ShapeDtypeStruct((2 * ny * q_width, nz * nx * rows), F32),
            jax.ShapeDtypeStruct((8 * outer, rows), F32),
        ],
        name="spread_attn",
    )(stacked)


def solution(mesh):
    sp_size = mesh.shape["sp"]
    dp_size = mesh.shape["dp"]
    side = round(dp_size**0.5)
    grid = jax.sharding.Mesh(mesh.devices.reshape(side, dp_size // side, sp_size // 2, 2), ("z", "y", "x", "c"))
    seq_spec = P(("z", "y"), ("x", "c"), None)
    seq_axes, mlp_axes = ("x", "c"), ("y", "c")
    mlp_size = grid.shape["y"] * 2
    mlp_outer = grid.shape["z"] * grid.shape["x"]
    inv_batch = 1.0 / dp_size

    def device_step(tokens, grad_out, norm_attn, w_query, w_key, w_value, w_out, norm_mlp, w_gate, w_up, w_down):
        x = tokens[0]
        dy = grad_out[0]
        n_local, dim = x.shape
        n_seq = n_local * sp_size
        q_width = w_query.shape[1] // sp_size
        k_width = w_key.shape[1] // sp_size
        ff_local = w_gate.shape[1] // mlp_size
        rows = dim // dp_size
        attn_blk = min(512, n_seq // 2)
        cos_all, sin_all = rope_tables(jnp.arange(n_seq))

        def to_heads(stacked):
            return lax.all_to_all(stacked, seq_axes, 0, 0, tiled=True)

        def gather(local, axes):
            return lax.all_gather(local, axes, axis=0, tiled=True)

        normed, unit_attn, inv_attn = norm_fwd(x, norm_attn)
        dy_full = gather(dy, mlp_axes)
        normed_full, qkv = gather_qkv(normed, w_query, w_key, w_value, sp_size, 3)
        _, lse, attn_tok = attn_fwd(qkv, sp_size // 2, 4)
        w_out_heads = w_out.reshape(sp_size, q_width, dim)
        projected = jnp.einsum("jte,jed->td", attn_tok, w_out_heads, preferred_element_type=F32)
        hidden = (x.astype(F32) + projected).astype(BF16)
        normed_mlp, unit_mlp, inv_mlp = norm_fwd(hidden, norm_mlp)
        m_full = gather(normed_mlp, mlp_axes)

        grad_m = mlp_grad_input(normed_mlp, dy, w_gate, w_up, w_down, min(512, w_gate.shape[1]))
        grad_hid_norm, g_norm_mlp = norm_bwd(grad_m, unit_mlp, inv_mlp, norm_mlp)
        grad_hidden = (dy.astype(F32) + grad_hid_norm).astype(BF16)
        grad_hidden_y = gather(grad_hidden, mlp_axes)
        attn_y = lax.all_to_all(attn_tok, mlp_axes, 0, 0, tiled=True).reshape(n_seq, q_width)

        g_mlp = mlp_ring(m_full, dy_full, w_gate, w_up, w_down, ff_local, inv_batch, "z", "x", side, mlp_axes, 1)
        g_mlp, late_hidden = lax.optimization_barrier((g_mlp, grad_hidden))
        g_mlp = gather(g_mlp, ("z", "x", "y", "c"))

        grad_attn = jnp.einsum("td,jed->jte", late_hidden, w_out_heads, preferred_element_type=F32).astype(BF16)
        grad_attn = to_heads(grad_attn).reshape(n_seq, q_width)
        g_out = tn(grad_hidden_y, attn_y).astype(BF16).reshape(mlp_outer, rows, q_width)
        g_out = ring_reduce(g_out, inv_batch, 1, "z", "x", 5)

        gqkv = attn_bwd(qkv, grad_attn, lse, cos_all, sin_all, attn_blk)
        gqkv_tok = to_heads(gqkv.reshape(sp_size, n_local, q_width + 2 * k_width))
        flat = lambda t: jnp.transpose(t, (1, 0, 2)).reshape(n_local, -1)
        grad_normed = (
            nt(flat(gqkv_tok[:, :, :q_width]), w_query)
            + nt(flat(gqkv_tok[:, :, q_width : q_width + k_width]), w_key)
            + nt(flat(gqkv_tok[:, :, q_width + k_width :]), w_value)
        ).astype(BF16)
        grad_tok_norm, g_norm_attn = norm_bwd(grad_normed, unit_attn, inv_attn, norm_attn)
        grad_tokens = (grad_hidden.astype(F32) + grad_tok_norm).astype(BF16)

        g_attn = tn(normed_full, gqkv).astype(BF16).reshape(dp_size, rows, q_width + 2 * k_width)
        gains = jnp.stack([g_norm_attn.reshape(dp_size, rows), g_norm_mlp.reshape(dp_size, rows)], axis=1)
        gains = jnp.pad(gains.astype(BF16), ((0, 0), (0, rows - 2), (0, 0)))
        g_attn = ring_reduce(jnp.concatenate([g_attn, gains], axis=2), inv_batch, 2, "z", "y", 2)
        g_attn = gather(jnp.concatenate([g_attn, g_out], axis=1), ("z", "y", "x", "c"))

        g_gate, g_up, g_down = spread_mlp(g_mlp, mlp_outer, mlp_size, ff_local)
        g_query, g_key, g_value, g_out, gains = spread_attn(g_attn, side, dp_size // side, sp_size, q_width, k_width)
        gains = gains.reshape(dp_size, 8, rows)
        return (
            grad_tokens[None],
            gains[:, 0].reshape(dim),
            g_query,
            g_key,
            g_value,
            g_out,
            gains[:, 1].reshape(dim),
            g_gate,
            g_up,
            g_down,
        )

    return jax.shard_map(device_step, mesh=grid, in_specs=(seq_spec, seq_spec) + (P(),) * 9, out_specs=(seq_spec,) + (P(),) * 9, check_vma=False)
```

profile of v0, /device:TPU:6, one launch (start us, length us, event | category | flops | bytes accessed | tf_op | source)
XLA Modules:
  0.0 815.9 jit_solution(11538238862036337700)
XLA Ops:
  8.6 1.5 fusion.24
  13.0 42.1 %gather_qkv.1 = (bf16[2048,2048]{1,0:T(8,128)(2,1)}, bf16[2048,512]{1,0:T(8,128)(2,1)}) custom-call(bf16[256,2048]{1,0:T(8,128)(2,1)} %fusion.21.x_ref, bf16[2048,2048]{1,0:T(8,128)(2,1)} %wq_ref.1, bf16[2048,1024]{1,0:T(8,128)(2,1)} %wk_ref.1, bf16[2048,1024]{1,0:T(8,128)(2,1)} %wv_ref.1, f32[8,128]{1,0:T(8,128)} %get-tuple-element.58.cos_blk, ...), custom_call_target="tpu_custom_call" | custom-call | flops 20000000000 | bytes 25165824 | tf_op jit(solution)/shard_map/gather_qkv/pallas_call | solution.py:192
  55.1 25.4 %attn_fwd.1 = (bf16[2048,256]{1,0:T(8,128)(2,1)}, f32[16,2048]{1,0:T(8,128)}, bf16[8,256,256]{2,1,0:T(8,128)(2,1)}) custom-call(bf16[2048,512]{1,0:T(8,128)(2,1)} %get-tuple-element.24.qkv_ref), custom_call_target="tpu_custom_call" | custom-call | flops 4294967296 | bytes 2097152 | tf_op jit(solution)/shard_map/attn_fwd/pallas_call | solution.py:308
  80.5 6.2 fusion.19
  89.1 43.7 %mlp_grad_input.1 = bf16[256,2048]{1,0:T(8,128)(2,1)} custom-call(bf16[256,2048]{1,0:T(8,128)(2,1)} %fusion.17.m_ref, bf16[256,2048]{1,0:T(8,128)(2,1)} %bitcast.62, bf16[2048,6144]{1,0:T(8,128)(2,1)} %wg_all.1, bf16[2048,6144]{1,0:T(8,128)(2,1)} %wu_all.1, bf16[6144,2048]{1,0:T(8,128)(2,1)} %wd_all.1), custom_call_target="tpu_custom_call" | custom-call | flops 32212254720 | bytes 75497472 | tf_op jit(solution)/shard_map/mlp_grad_input/pallas_call | solution.py:443
  132.8 2.2 fusion.20
  135.0 1.8 fusion.16
  136.8 7.0 all-to-all-start.2
  143.8 5.4 fusion.28
  149.2 46.0 %all-gather.15.cloned.1.call-done = bf16[1,2048,2048]{2,1,0:T(8,128)(2,1)} async-done(((bf16[1,256,2048]{2,1,0:T(8,128)(2,1)}), bf16[1,2048,2048]{2,1,0:T(8,128)(2,1)}) %all-gather.15.cloned.1.call-update) | async-done | bytes 8388624 | tf_op jit(solution)/shard_map/all_gather | solution.py:818
  195.2 101.0 %mlp_ring.1 = bf16[2304,128]{1,0:T(8,128)(2,1)} custom-call(bf16[2048,2048]{1,0:T(8,128)(2,1)} %all-gather.7.cloned.1.call-done.m_ref, bf16[2048,2048]{1,0:T(8,128)(2,1)} %bitcast.76, bf16[2048,6144]{1,0:T(8,128)(2,1)} %wg_all.1, bf16[2048,6144]{1,0:T(8,128)(2,1)} %wu_all.1, bf16[6144,2048]{1,0:T(8,128)(2,1)} %wd_all.1), custom_call_target="tpu_custom_call" | custom-call | flops 57982058496 | bytes 16777216 | tf_op jit(solution)/shard_map/mlp_ring/pallas_call | solution.py:665
  296.2 6.7 fusion.25
  302.9 6.3 all-to-all-start
  309.3 3.5 pad_maximum_fusion.1
  312.7 7.1 convolution_convert_fusion.1
  319.8 3.3 all-to-all-done
  323.2 23.9 %attn_bwd.1 = bf16[2048,512]{1,0:T(8,128)(2,1)} custom-call(bf16[2048,512]{1,0:T(8,128)(2,1)} %get-tuple-element.24.qkv_ref, bf16[2048,256]{1,0:T(8,128)(2,1)} %bitcast.8.do_ref, f32[16,2048]{1,0:T(8,128)} %get-tuple-element.27.lse_ref, f32[2048,128]{1,0:T(8,128)} %get-tuple-element.62.cos_ref, f32[2048,128]{1,0:T(8,128)} %get-tuple-element.63.sin_ref), custom_call_target="tpu_custom_call" | custom-call | flops 10737418240 | bytes 4194304 | tf_op jit(solution)/shard_map/attn_bwd/pallas_call | solution.py:391
  347.1 3.9 copy.21
  351.0 6.4 all-to-all-start.1
  357.6 44.1 %ring_reduce.3 = bf16[128,256]{1,0:T(8,128)(2,1)} custom-call(bf16[4,4,128,256]{3,2,1,0:T(8,128)(2,1)} %bitcast.77), custom_call_target="tpu_custom_call" | custom-call | flops 40000000000 | bytes 1048576 | tf_op jit(solution)/shard_map/ring_reduce/pallas_call | solution.py:706
  401.8 9.4 %convolution_convert_fusion = bf16[2048,512]{1,0:T(8,128)(2,1)} fusion(bf16[2048,2048]{1,0:T(8,128)(2,1)} %get-tuple-element.28, bf16[2048,512]{1,0:T(8,128)(2,1)S(1)} %copy-done.7), kind=kOutput, calls=%fused_computation.7 | convolution fusion | flops 4296015872 | bytes 12582912 | tf_op jit(solution)/shard_map/dot_general | solution.py:31
  412.5 5.9 fusion.33
  422.3 1.9 fusion.23
  424.3 1.8 pad_maximum_fusion.g_ref
  426.0 28.9 %ring_reduce.2 = bf16[128,640]{1,0:T(8,128)(2,1)} custom-call(bf16[4,4,128,640]{3,2,1,0:T(8,128)(2,1)} %pad_maximum_fusion.g_ref), custom_call_target="tpu_custom_call" | custom-call | flops 40000000000 | bytes 2621440 | tf_op jit(solution)/shard_map/ring_reduce/pallas_call | solution.py:706
  454.9 1.6 pad_maximum_fusion.3
  457.2 1.7 fusion.26
  458.9 96.8 %all-gather.11.cloned.1.call-done.in_ref = bf16[16384,896]{1,0:T(8,128)(2,1)} async-done(((bf16[128,896]{1,0:T(8,128)(2,1)}), bf16[16384,896]{1,0:T(8,128)(2,1)}) %all-gather.11.cloned.1.call-update) | async-done | bytes 29360144 | tf_op jit(solution)/shard_map/all_gather | solution.py:818
  555.7 28.6 %spread_attn.1 = (f32[2048,2048]{1,0:T(8,128)}, f32[2048,1024]{1,0:T(8,128)}, f32[2048,1024]{1,0:T(8,128)}, f32[2048,2048]{1,0:T(8,128)}, f32[128,128]{1,0:T(8,128)}) custom-call(bf16[16384,896]{1,0:T(8,128)(2,1)} %all-gather.11.cloned.1.call-done.in_ref), custom_call_target="tpu_custom_call" | custom-call | flops 14680064 | bytes 88080384 | tf_op jit(solution)/shard_map/spread_attn/pallas_call | solution.py:767
  584.3 1.5 fusion.32
  585.8 151.4 %all-gather.13.cloned.1.call-done.in_ref = bf16[294912,128]{1,0:T(8,128)(2,1)} async-done(((bf16[2304,128]{1,0:T(8,128)(2,1)}), bf16[294912,128]{1,0:T(8,128)(2,1)}) %all-gather.13.cloned.1.call-update) | async-done | bytes 75497488 | tf_op jit(solution)/shard_map/all_gather | solution.py:818
  737.2 71.9 %spread_mlp.1 = (f32[2048,6144]{1,0:T(8,128)}, f32[2048,6144]{1,0:T(8,128)}, f32[6144,2048]{1,0:T(8,128)}) custom-call(bf16[294912,128]{1,0:T(8,128)(2,1)} %all-gather.13.cloned.1.call-done.in_ref), custom_call_target="tpu_custom_call" | custom-call | flops 37748736 | bytes 226492416 | tf_op jit(solution)/shard_map/spread_mlp/pallas_call | solution.py:729
  (66 shorter events, 12.6 us)
Async XLA Ops:
  7.2 3.0 copy-start
  7.2 142.0 %all-gather.7.cloned.1.call-start = ((), (), s32[]{:S(2)}) async-start(), calls=%async_computation.3 | async-start | bytes 9437184 | tf_op jit(solution)/shard_map/all_gather | solution.py:818
  8.6 3.7 copy-start.8
  10.2 2.8 copy-start.11
  80.5 6.2 copy-start.13
  88.1 107.1 %all-gather.15.cloned.1.call-start = ((), (), s32[]{:S(2)}) async-start(), calls=%async_computation.7 | async-start | bytes 9437184 | tf_op jit(solution)/shard_map/all_gather | solution.py:818
  88.8 223.9 %all-gather.9.cloned.1.call-start = ((), (), s32[]{:S(2)}) async-start(), calls=%async_computation.4 | async-start | bytes 9437184 | tf_op jit(solution)/shard_map/all_gather | solution.py:818
  132.8 2.2 copy-start.4
  132.8 2.2 copy-start.5
  136.8 166.1 %all-to-all-start.2 = ((bf16[8,256,256]{2,1,0:T(8,128)(2,1)}), bf16[8,256,256]{2,1,0:T(8,128)(2,1)}, u32[]{:S(2)}, u32[]{:S(2)}) async-start(bf16[8,256,256]{2,1,0:T(8,128)(2,1)} %get-tuple-element.25), calls=%async_computation.2 | async-start | bytes 2097152 | tf_op jit(solution)/shard_map/all_to_all | solution.py:834
  195.2 101.0 %copy-start.2 = (bf16[256,2048]{1,0:T(8,128)(2,1)S(1)}, bf16[256,2048]{1,0:T(8,128)(2,1)}, u32[]{:S(2)}) copy-start(bf16[256,2048]{1,0:T(8,128)(2,1)} %fusion.16) | copy-start | bytes 3145732
  302.9 20.2 %all-to-all-start = ((bf16[8,256,256]{2,1,0:T(8,128)(2,1)}), bf16[8,256,256]{2,1,0:T(8,128)(2,1)}, u32[]{:S(2)}, u32[]{:S(2)}) async-start(bf16[8,256,256]{2,1,0:T(8,128)(2,1)} %fusion.25), calls=%async_computation | async-start | bytes 2097152 | tf_op jit(solution)/shard_map/all_to_all | solution.py:815
  351.0 60.2 %all-to-all-start.1 = ((bf16[8,256,512]{1,2,0:T(8,128)(2,1)}), bf16[8,256,512]{1,2,0:T(8,128)(2,1)}, u32[]{:S(2)}, u32[]{:S(2)}) async-start(bf16[8,256,512]{1,2,0:T(8,128)(2,1)} %copy.21), calls=%async_computation.1 | async-start | bytes 4194304 | tf_op jit(solution)/shard_map/all_to_all | solution.py:815
  357.4 198.3 %all-gather.11.cloned.1.call-start = ((), (), s32[]{:S(2)}) async-start(), calls=%async_computation.5 | async-start | bytes 29589504 | tf_op jit(solution)/shard_map/all_gather | solution.py:818
  357.6 44.2 %copy-start.7 = (bf16[2048,512]{1,0:T(8,128)(2,1)S(1)}, bf16[2048,512]{1,0:T(8,128)(2,1)}, u32[]{:S(2)}) copy-start(bf16[2048,512]{1,0:T(8,128)(2,1)} %attn_bwd.1) | copy-start | bytes 6291460
  412.5 7.2 copy-start.3
  419.7 1.4 copy-start.1
  419.7 1.4 copy-start.9
  419.7 1.4 copy-start.12
  419.8 2.5 copy-start.14
  422.3 2.0 copy-start.6
  426.0 28.9 %copy-start.10 = (bf16[128,256]{1,0:T(8,128)(2,1)S(1)}, bf16[128,256]{1,0:T(8,128)(2,1)}, u32[]{:S(2)}) copy-start(bf16[128,256]{1,0:T(8,128)(2,1)} %ring_reduce.3) | copy-start | bytes 196612
  456.6 280.7 %all-gather.13.cloned.1.call-start = ((), (), s32[]{:S(2)}) async-start(), calls=%async_computation.6 | async-start | bytes 76087296 | tf_op jit(solution)/shard_map/all_gather | solution.py:818
Sparse Core Ops, SparseCore 0:
  88.2 53.4 all-gather.6
  143.3 51.7 all-gather.14
  197.5 49.2 all-gather.8
  456.7 98.9 all-gather.10
  558.6 178.5 all-gather.12
where the time goes:
time: 824 us; the launch traced here: 816 us
  Pallas kernels  410 us (50%)
  waiting for transfers between devices  299 us (36%)
  matrix products  38.5 us (5%)
  other arithmetic  24.9 us (3%)
  starting transfers between devices  20.3 us (2%)
  between operations  14.4 us (2%)
  local copies, waits for them, and re-layouts  9.36 us (1%)
    all_gather x5, waiting for transfers between devices, gather(): return lax.all_gather(local, axes, axis=0, tiled=True)  294 us
    pallas_call x1, Pallas kernels, mlp_ring(): pl.pallas_call(functools.partial(mlp_ring_kernel, n, subs, scale, blocks,...  101 us
    pallas_call x2, Pallas kernels, ring_reduce(): pl.pallas_call(functools.partial(ring_reduce_kernel, n, subs, scale, slow...  73 us
    pallas_call x1, Pallas kernels, spread_mlp(): call(functools.partial(spread_mlp_kernel, groups, ff_local, min(256, ff_l...  71.9 us
    pallas_call x1, Pallas kernels, mlp_grad_input(): call(mlp_kernel, 5 * 2 * tok * dim * width, 3 * 2 * dim * width, grid=(wi...  43.7 us
    pallas_call x1, Pallas kernels, gather_qkv(): pl.pallas_call(gather_qkv_kernel, in_specs=[vmem, anywhere, anywhere, any...  42.1 us
    pallas_call x1, Pallas kernels, spread_attn(): call(functools.partial(spread_attn_kernel, groups, q_width, k_width), tot...  28.6 us
    pallas_call x1, Pallas kernels, attn_fwd(): pl.pallas_call(functools.partial(attn_fwd_kernel, blk, n_q), grid=(steps,...  25.4 us
  transfers between devices with their start and end apart: 8, of which 4 were waited for; matrix products, arithmetic and copies ran while one was open for 5% of the time, Pallas kernels for 27%

commit v1 on v0

--- a/solution.py
+++ b/solution.py
@@ -555,7 +555,7 @@
         ] + [pltpu.SemaphoreType.DMA((blocks, 4, n - 1, subs))] * 4
 
 
-def mlp_ring_kernel(n, subs, scale, blocks, slow, fast, group, m_ref, dy_ref, wg_all, wu_all, wd_all, out_ref, wg_buf, wu_buf, wd_buf, w_sems, grads_ref, act_ref, g_ref, *scratch):
+def mlp_ring_kernel(n, subs, scale, blocks, slow, fast, group, m_all, dy_all, wg_all, wu_all, wd_all, out_ref, m_ref, dy_ref, in_sems, wg_buf, wu_buf, wd_buf, w_sems, grads_ref, act_ref, g_ref, *scratch):
     step = pl.program_id(0)
     seq, dim = m_ref.shape
     width = act_ref.shape[0]
@@ -575,9 +575,15 @@
             pltpu.make_async_copy(wd_all.at[mine, :], wd_buf.at[slot], w_sems.at[slot, 2]),
         ]
 
+    def tokens(i):
+        return [
+            pltpu.make_async_copy(m_all.at[at(i, blk), :], m_ref.at[at(i, blk), :], in_sems.at[0, i]),
+            pltpu.make_async_copy(dy_all.at[at(i, blk), :], dy_ref.at[at(i, blk), :], in_sems.at[1, i]),
+        ]
+
     @pl.when(step == 0)
     def _():
-        for load in loads(0):
+        for load in loads(0) + [load for i in range(tiles) for load in tokens(i)]:
             load.start()
         ring.arrive()
         ring.meet()
@@ -597,7 +603,7 @@
     hops = [functools.partial(ring.hop1, t=t) for t in range(n - 1)]
     hops += [functools.partial(ring.hop2, t=t, scale=scale, store=store) for t in range(n - 1)]
     slots = 2 * tiles
-    delays = [3 * t + 4 if t < n - 1 else 3 * n + 2 * (t - n + 1) for t in range(2 * (n - 1))]
+    delays = [3 * t + 3 if t < n - 1 else 3 * n - 1 + 2 * (t - n + 1) for t in range(2 * (n - 1))]
 
     def events(slot):
         for hop, delay in zip(hops, delays):
@@ -609,6 +615,11 @@
                 hop(block)
 
     def forward(i):
+        @pl.when(step == 0)
+        def _():
+            for load in tokens(i):
+                load.wait()
+
         m, dy = m_ref[at(i, blk), :], dy_ref[at(i, blk), :]
         grad_act = nt(dy, wd_ref[...]).astype(BF16).astype(F32)
         act, grad_gate, grad_up = act_grads(nn(m, wg_ref[...]), nn(m, wu_ref[...]), grad_act)
@@ -660,14 +671,16 @@
     blocks = ff // width
     subs = 2
     rows = dim // (n * n)
-    once = lambda shape: pl.BlockSpec(shape, lambda j: (0, 0), pipeline_mode=pl.Buffered(1))
     anywhere = pl.BlockSpec(memory_space=pl.ANY)
     return pl.pallas_call(
         functools.partial(mlp_ring_kernel, n, subs, scale, blocks, slow, fast, group),
         grid=(blocks,),
-        in_specs=[once((seq, dim)), once((seq, dim)), anywhere, anywhere, anywhere],
+        in_specs=[anywhere] * 5,
         out_specs=pl.BlockSpec((3 * ff, rows), lambda j: (0, 0)),
         scratch_shapes=[
+            pltpu.VMEM((seq, dim), BF16),
+            pltpu.VMEM((seq, dim), BF16),
+            pltpu.SemaphoreType.DMA((2, 4)),
             pltpu.VMEM((2, dim, width), BF16),
             pltpu.VMEM((2, dim, width), BF16),
             pltpu.VMEM((2, width, dim), BF16),
@@ -746,14 +759,14 @@
     rows = q_ref.shape[0]
     gain = None
     for g in range(groups):
-        piece = in_ref[g * rows : (g + 1) * rows, :].astype(F32)
+        first = g * (rows + 8)
+        piece = in_ref[first : first + rows, :].astype(F32)
         q_ref[:, g * q_width : (g + 1) * q_width] = piece[:, :q_width]
         k_ref[:, g * k_width : (g + 1) * k_width] = piece[:, q_width : q_width + k_width]
         v_ref[:, g * k_width : (g + 1) * k_width] = piece[:, q_width + k_width : q_width + 2 * k_width]
-        gain_at, o_at = q_width + 2 * k_width, q_width + 2 * k_width + rows
         block, core = g // 2, g % 2
-        o_ref[core * q_width : (core + 1) * q_width, block * rows : (block + 1) * rows] = jnp.transpose(piece[:, o_at:])
-        part = piece[:8, gain_at:o_at]
+        o_ref[core * q_width : (core + 1) * q_width, block * rows : (block + 1) * rows] = jnp.transpose(piece[:, q_width + 2 * k_width :])
+        part = in_ref[first + rows : first + rows + 8, :rows].astype(F32)
         gain = part if gain is None else gain + part
     gain_ref[...] = gain
 
@@ -761,7 +774,7 @@
 def spread_attn(stacked, nz, ny, groups, q_width, k_width):
     total, row_width = stacked.shape
     outer = nz * ny
-    rows = total // (outer * groups)
+    rows = total // (outer * groups) - 8
     dim = rows * outer
     nx = groups // 2
     return call(
@@ -769,7 +782,7 @@
         total * row_width,
         total * row_width * 6,
         grid=(outer,),
-        in_specs=[pl.BlockSpec((groups * rows, row_width), lambda o: (o, 0))],
+        in_specs=[pl.BlockSpec((total // outer, row_width), lambda o: (o, 0))],
         out_specs=[
             pl.BlockSpec((rows, groups * q_width), lambda o: (o, 0)),
             pl.BlockSpec((rows, groups * k_width), lambda o: (o, 0)),
@@ -857,7 +870,10 @@
         gains = jnp.stack([g_norm_attn.reshape(dp_size, rows), g_norm_mlp.reshape(dp_size, rows)], axis=1)
         gains = jnp.pad(gains.astype(BF16), ((0, 0), (0, rows - 2), (0, 0)))
         g_attn = ring_reduce(jnp.concatenate([g_attn, gains], axis=2), inv_batch, 2, "z", "y", 2)
-        g_attn = gather(jnp.concatenate([g_attn, g_out], axis=1), ("z", "y", "x", "c"))
+        gain_at = q_width + 2 * k_width
+        gains = jnp.pad(g_attn[:8, gain_at:], ((0, 0), (0, 2 * (q_width + k_width) - rows)))
+        g_attn = jnp.concatenate([jnp.concatenate([g_attn[:, :gain_at], g_out], axis=1), gains], axis=0)
+        g_attn = gather(g_attn, ("z", "y", "x", "c"))
 
         g_gate, g_up, g_down = spread_mlp(g_mlp, mlp_outer, mlp_size, ff_local)
         g_query, g_key, g_value, g_out, gains = spread_attn(g_attn, side, dp_size // side, sp_size, q_width, k_width)

time: 824 us -> 818 us (level)
  transfers between devices with their start and end apart: 8 -> 8, of which waited for: 4 -> 4; matrix products, arithmetic and copies ran while one was open for 5% -> 5% of each run, Pallas kernels for 27% -> 26%
where the time goes in v1:
time: 818 us; the launch traced here: 810 us
  Pallas kernels  406 us (50%)
  waiting for transfers between devices  296 us (36%)
  matrix products  38.5 us (5%)
  other arithmetic  23.9 us (3%)
  starting transfers between devices  20.4 us (2%)
  between operations  14.4 us (2%)
  local copies, waits for them, and re-layouts  11 us (1%)
    all_gather x5, waiting for transfers between devices, gather(): return lax.all_gather(local, axes, axis=0, tiled=True)  292 us
    pallas_call x1, Pallas kernels, mlp_ring(): pl.pallas_call(functools.partial(mlp_ring_kernel, n, subs, scale, blocks,...  98.4 us
    pallas_call x2, Pallas kernels, ring_reduce(): pl.pallas_call(functools.partial(ring_reduce_kernel, n, subs, scale, slow...  72.9 us
    pallas_call x1, Pallas kernels, spread_mlp(): call(functools.partial(spread_mlp_kernel, groups, ff_local, min(256, ff_l...  71.9 us
    pallas_call x1, Pallas kernels, mlp_grad_input(): call(mlp_kernel, 5 * 2 * tok * dim * width, 3 * 2 * dim * width, grid=(wi...  43.7 us
    pallas_call x1, Pallas kernels, gather_qkv(): pl.pallas_call(gather_qkv_kernel, in_specs=[vmem, anywhere, anywhere, any...  42.1 us
    pallas_call x1, Pallas kernels, spread_attn(): call(functools.partial(spread_attn_kernel, groups, q_width, k_width), tot...  27.3 us
    pallas_call x1, Pallas kernels, attn_fwd(): pl.pallas_call(functools.partial(attn_fwd_kernel, blk, n_q), grid=(steps,...  25.4 us
  transfers between devices with their start and end apart: 8, of which 4 were waited for; matrix products, arithmetic and copies ran while one was open for 5% of the time, Pallas kernels for 26%

profile of v1, /device:TPU:6, one launch (start us, length us, event | category | flops | bytes accessed | tf_op | source)
XLA Modules:
  0.0 810.0 jit_solution(6987138185775647129)
XLA Ops:
  8.6 1.5 fusion.24
  13.0 42.1 %gather_qkv.1 = (bf16[2048,2048]{1,0:T(8,128)(2,1)}, bf16[2048,512]{1,0:T(8,128)(2,1)}) custom-call(bf16[256,2048]{1,0:T(8,128)(2,1)} %fusion.21.x_ref, bf16[2048,2048]{1,0:T(8,128)(2,1)} %wq_ref.1, bf16[2048,1024]{1,0:T(8,128)(2,1)} %wk_ref.1, bf16[2048,1024]{1,0:T(8,128)(2,1)} %wv_ref.1, f32[8,128]{1,0:T(8,128)} %get-tuple-element.58.cos_blk, ...), custom_call_target="tpu_custom_call" | custom-call | flops 20000000000 | bytes 25165824 | tf_op jit(solution)/shard_map/gather_qkv/pallas_call | solution.py:192
  55.1 25.4 %attn_fwd.1 = (bf16[2048,256]{1,0:T(8,128)(2,1)}, f32[16,2048]{1,0:T(8,128)}, bf16[8,256,256]{2,1,0:T(8,128)(2,1)}) custom-call(bf16[2048,512]{1,0:T(8,128)(2,1)} %get-tuple-element.24.qkv_ref), custom_call_target="tpu_custom_call" | custom-call | flops 4294967296 | bytes 2097152 | tf_op jit(solution)/shard_map/attn_fwd/pallas_call | solution.py:308
  80.5 6.2 fusion.19
  89.1 43.7 %mlp_grad_input.1 = bf16[256,2048]{1,0:T(8,128)(2,1)} custom-call(bf16[256,2048]{1,0:T(8,128)(2,1)} %fusion.17.m_ref, bf16[256,2048]{1,0:T(8,128)(2,1)} %bitcast.62, bf16[2048,6144]{1,0:T(8,128)(2,1)} %wg_all.1, bf16[2048,6144]{1,0:T(8,128)(2,1)} %wu_all.1, bf16[6144,2048]{1,0:T(8,128)(2,1)} %wd_all.1), custom_call_target="tpu_custom_call" | custom-call | flops 32212254720 | bytes 75497472 | tf_op jit(solution)/shard_map/mlp_grad_input/pallas_call | solution.py:443
  132.8 2.2 fusion.20
  135.0 1.8 fusion.16
  136.8 7.0 all-to-all-start.2
  143.8 5.4 fusion.29
  149.2 46.0 %all-gather.15.cloned.1.call-done = bf16[1,2048,2048]{2,1,0:T(8,128)(2,1)} async-done(((bf16[1,256,2048]{2,1,0:T(8,128)(2,1)}), bf16[1,2048,2048]{2,1,0:T(8,128)(2,1)}) %all-gather.15.cloned.1.call-update) | async-done | bytes 8388624 | tf_op jit(solution)/shard_map/all_gather | solution.py:831
  195.2 98.4 %mlp_ring.1 = bf16[2304,128]{1,0:T(8,128)(2,1)} custom-call(bf16[2048,2048]{1,0:T(8,128)(2,1)} %all-gather.7.cloned.1.call-done.m_all, bf16[2048,2048]{1,0:T(8,128)(2,1)} %bitcast.76, bf16[2048,6144]{1,0:T(8,128)(2,1)} %wg_all.1, bf16[2048,6144]{1,0:T(8,128)(2,1)} %wu_all.1, bf16[6144,2048]{1,0:T(8,128)(2,1)} %wd_all.1), custom_call_target="tpu_custom_call" | custom-call | flops 57982058496 | bytes 16777216 | tf_op jit(solution)/shard_map/mlp_ring/pallas_call | solution.py:675
  293.6 6.7 fusion.25
  300.3 6.4 all-to-all-start
  306.8 3.5 pad_maximum_fusion.1
  310.2 7.1 convolution_convert_fusion.1
  317.3 3.3 all-to-all-done
  320.6 23.9 %attn_bwd.1 = bf16[2048,512]{1,0:T(8,128)(2,1)} custom-call(bf16[2048,512]{1,0:T(8,128)(2,1)} %get-tuple-element.24.qkv_ref, bf16[2048,256]{1,0:T(8,128)(2,1)} %bitcast.8.do_ref, f32[16,2048]{1,0:T(8,128)} %get-tuple-element.27.lse_ref, f32[2048,128]{1,0:T(8,128)} %get-tuple-element.62.cos_ref, f32[2048,128]{1,0:T(8,128)} %get-tuple-element.63.sin_ref), custom_call_target="tpu_custom_call" | custom-call | flops 10737418240 | bytes 4194304 | tf_op jit(solution)/shard_map/attn_bwd/pallas_call | solution.py:391
  344.6 3.9 copy.21
  348.5 6.4 all-to-all-start.1
  355.1 44.3 %ring_reduce.3 = bf16[128,256]{1,0:T(8,128)(2,1)} custom-call(bf16[4,4,128,256]{3,2,1,0:T(8,128)(2,1)} %bitcast.77), custom_call_target="tpu_custom_call" | custom-call | flops 40000000000 | bytes 1048576 | tf_op jit(solution)/shard_map/ring_reduce/pallas_call | solution.py:719
  399.4 9.4 %convolution_convert_fusion = bf16[2048,512]{1,0:T(8,128)(2,1)} fusion(bf16[2048,2048]{1,0:T(8,128)(2,1)} %get-tuple-element.28, bf16[2048,512]{1,0:T(8,128)(2,1)S(1)} %copy-done.7), kind=kOutput, calls=%fused_computation.7 | convolution fusion | flops 4296015872 | bytes 12582912 | tf_op jit(solution)/shard_map/dot_general | solution.py:31
  410.1 5.9 fusion.35
  417.4 1.3 convolution_add_fusion.1
  419.9 1.9 fusion.23
  421.9 1.8 pad_maximum_fusion.g_ref
  423.7 28.6 %ring_reduce.2 = bf16[128,640]{1,0:T(8,128)(2,1)} custom-call(bf16[4,4,128,640]{3,2,1,0:T(8,128)(2,1)} %pad_maximum_fusion.g_ref), custom_call_target="tpu_custom_call" | custom-call | flops 40000000000 | bytes 2621440 | tf_op jit(solution)/shard_map/ring_reduce/pallas_call | solution.py:719
  455.2 1.7 fusion.26
  457.0 92.8 %all-gather.11.cloned.1.call-done.in_ref = bf16[17408,768]{1,0:T(8,128)(2,1)} async-done(((bf16[136,768]{1,0:T(8,128)(2,1)}), bf16[17408,768]{1,0:T(8,128)(2,1)}) %all-gather.11.cloned.1.call-update) | async-done | bytes 26738704 | tf_op jit(solution)/shard_map/all_gather | solution.py:831
  549.8 27.3 %spread_attn.1 = (f32[2048,2048]{1,0:T(8,128)}, f32[2048,1024]{1,0:T(8,128)}, f32[2048,1024]{1,0:T(8,128)}, f32[2048,2048]{1,0:T(8,128)}, f32[128,128]{1,0:T(8,128)}) custom-call(bf16[17408,768]{1,0:T(8,128)(2,1)} %all-gather.11.cloned.1.call-done.in_ref), custom_call_target="tpu_custom_call" | custom-call | flops 13369344 | bytes 80216064 | tf_op jit(solution)/shard_map/spread_attn/pallas_call | solution.py:780
  577.1 1.5 fusion.34
  578.6 152.7 %all-gather.13.cloned.1.call-done.in_ref = bf16[294912,128]{1,0:T(8,128)(2,1)} async-done(((bf16[2304,128]{1,0:T(8,128)(2,1)}), bf16[294912,128]{1,0:T(8,128)(2,1)}) %all-gather.13.cloned.1.call-update) | async-done | bytes 75497488 | tf_op jit(solution)/shard_map/all_gather | solution.py:831
  731.4 71.9 %spread_mlp.1 = (f32[2048,6144]{1,0:T(8,128)}, f32[2048,6144]{1,0:T(8,128)}, f32[6144,2048]{1,0:T(8,128)}) custom-call(bf16[294912,128]{1,0:T(8,128)(2,1)} %all-gather.13.cloned.1.call-done.in_ref), custom_call_target="tpu_custom_call" | custom-call | flops 37748736 | bytes 226492416 | tf_op jit(solution)/shard_map/spread_mlp/pallas_call | solution.py:742
  (68 shorter events, 13.6 us)
Async XLA Ops:
  7.2 3.0 copy-start
  7.2 142.0 %all-gather.7.cloned.1.call-start = ((), (), s32[]{:S(2)}) async-start(), calls=%async_computation.3 | async-start | bytes 9437184 | tf_op jit(solution)/shard_map/all_gather | solution.py:831
  8.6 3.7 copy-start.8
  10.2 2.8 copy-start.11
  80.5 6.2 copy-start.13
  88.1 107.1 %all-gather.15.cloned.1.call-start = ((), (), s32[]{:S(2)}) async-start(), calls=%async_computation.7 | async-start | bytes 9437184 | tf_op jit(solution)/shard_map/all_gather | solution.py:831
  88.8 221.4 %all-gather.9.cloned.1.call-start = ((), (), s32[]{:S(2)}) async-start(), calls=%async_computation.4 | async-start | bytes 9437184 | tf_op jit(solution)/shard_map/all_gather | solution.py:831
  132.8 2.2 copy-start.4
  132.8 2.2 copy-start.5
  136.8 163.5 %all-to-all-start.2 = ((bf16[8,256,256]{2,1,0:T(8,128)(2,1)}), bf16[8,256,256]{2,1,0:T(8,128)(2,1)}, u32[]{:S(2)}, u32[]{:S(2)}) async-start(bf16[8,256,256]{2,1,0:T(8,128)(2,1)} %get-tuple-element.25), calls=%async_computation.2 | async-start | bytes 2097152 | tf_op jit(solution)/shard_map/all_to_all | solution.py:847
  195.2 98.4 %copy-start.2 = (bf16[256,2048]{1,0:T(8,128)(2,1)S(1)}, bf16[256,2048]{1,0:T(8,128)(2,1)}, u32[]{:S(2)}) copy-start(bf16[256,2048]{1,0:T(8,128)(2,1)} %fusion.16) | copy-start | bytes 3145732
  300.3 20.3 %all-to-all-start = ((bf16[8,256,256]{2,1,0:T(8,128)(2,1)}), bf16[8,256,256]{2,1,0:T(8,128)(2,1)}, u32[]{:S(2)}, u32[]{:S(2)}) async-start(bf16[8,256,256]{2,1,0:T(8,128)(2,1)} %fusion.25), calls=%async_computation | async-start | bytes 2097152 | tf_op jit(solution)/shard_map/all_to_all | solution.py:828
  348.5 60.3 %all-to-all-start.1 = ((bf16[8,256,512]{1,2,0:T(8,128)(2,1)}), bf16[8,256,512]{1,2,0:T(8,128)(2,1)}, u32[]{:S(2)}, u32[]{:S(2)}) async-start(bf16[8,256,512]{1,2,0:T(8,128)(2,1)} %copy.21), calls=%async_computation.1 | async-start | bytes 4194304 | tf_op jit(solution)/shard_map/all_to_all | solution.py:828
  354.9 194.9 %all-gather.11.cloned.1.call-start = ((), (), s32[]{:S(2)}) async-start(), calls=%async_computation.5 | async-start | bytes 26947584 | tf_op jit(solution)/shard_map/all_gather | solution.py:831
  355.1 44.3 %copy-start.7 = (bf16[2048,512]{1,0:T(8,128)(2,1)S(1)}, bf16[2048,512]{1,0:T(8,128)(2,1)}, u32[]{:S(2)}) copy-start(bf16[2048,512]{1,0:T(8,128)(2,1)} %attn_bwd.1) | copy-start | bytes 6291460
  410.1 7.2 copy-start.3
  417.3 1.4 copy-start.1
  417.3 1.4 copy-start.9
  417.4 1.4 copy-start.12
  417.4 2.5 copy-start.14
  419.9 2.0 copy-start.6
  423.7 30.3 %copy-start.10 = (bf16[128,256]{1,0:T(8,128)(2,1)S(1)}, bf16[128,256]{1,0:T(8,128)(2,1)}, u32[]{:S(2)}) copy-start(bf16[128,256]{1,0:T(8,128)(2,1)} %ring_reduce.3) | copy-start | bytes 196612
  454.6 276.7 %all-gather.13.cloned.1.call-start = ((), (), s32[]{:S(2)}) async-start(), calls=%async_computation.6 | async-start | bytes 76087296 | tf_op jit(solution)/shard_map/all_gather | solution.py:831
Sparse Core Ops, SparseCore 0:
  88.2 53.4 all-gather.6
  143.3 51.7 all-gather.14
  197.5 49.2 all-gather.8
  454.8 94.9 all-gather.10
  552.8 178.5 all-gather.12

commit v2 on v1

--- a/solution.py
+++ b/solution.py
@@ -324,7 +324,7 @@
     )(qkv)
 
 
-def attn_bwd_kernel(blk, n_q, qkv_ref, do_ref, lse_ref, cos_ref, sin_ref, out_ref, dk_scr, dv_scr, *scrs):
+def attn_bwd_kernel(blk, n_q, qkv_ref, do_ref, lse_ref, cos_blk, sin_blk, cos_row, sin_row, out_ref, dk_scr, dv_scr, *scrs):
     i, steps = pl.program_id(0), pl.num_programs(0)
     scale = HEAD_DIM**-0.5
     coef = scale * math.log2(math.e)
@@ -341,13 +341,11 @@
         dk_scr[...] = jnp.zeros_like(dk_scr)
         dv_scr[...] = jnp.zeros_like(dv_scr)
 
-    def prob_step(j, dots, masked):
+    def prob_step(j, dots):
         key, value = qkv_ref[at(j), k_at:v_at], qkv_ref[at(j), v_at : v_at + HEAD_DIM]
         new, dv = [], dv_scr[at(j), :]
         for h in range(n_q):
-            p = jnp.exp2(nt(key, qs[h]) * coef - lses[h])
-            if masked:
-                p = jnp.where(causal, p, 0.0)
+            p = jnp.where(causal | (j < i), jnp.exp2(nt(key, qs[h]) * coef - lses[h]), 0.0)
             dp = nt(value, dos[h]).astype(BF16)
             p_scrs[h][at(j), :] = p
             dp_scrs[h][at(j), :] = dp
@@ -356,8 +354,7 @@
         dv_scr[at(j), :] = dv
         return tuple(new)
 
-    dots = lax.fori_loop(0, i, lambda j, t: prob_step(j, t, False), tuple(jnp.zeros((8, blk), F32) for _ in range(n_q)))
-    dots = prob_step(i, dots, True)
+    dots = lax.fori_loop(0, i + 1, prob_step, tuple(jnp.zeros((8, blk), F32) for _ in range(n_q)))
     row_dot = [jnp.sum(t, axis=0, keepdims=True) for t in dots]
 
     def grad_step(j, accs):
@@ -371,21 +368,27 @@
         return tuple(new)
 
     accs = lax.fori_loop(0, i + 1, grad_step, tuple(jnp.zeros((blk, HEAD_DIM), F32) for _ in range(n_q)))
-    unrope = lambda g, sl: rope(g.astype(BF16).astype(F32), cos_ref[sl, :], -sin_ref[sl, :]).astype(BF16)
+
+    def unrope(grad, j):
+        cos_b, sin_b = cos_blk[pl.ds(j, 1), :], sin_blk[pl.ds(j, 1), :]
+        cos = cos_b * cos_row[...] - sin_b * sin_row[...]
+        sin = sin_b * cos_row[...] + cos_b * sin_row[...]
+        return rope(grad.astype(BF16).astype(F32), cos, -sin).astype(BF16)
+
     for h in range(n_q):
-        out_ref[at(i), h * HEAD_DIM : (h + 1) * HEAD_DIM] = unrope(accs[h], at(i))
+        out_ref[at(i), h * HEAD_DIM : (h + 1) * HEAD_DIM] = unrope(accs[h], i)
 
     @pl.when(i == steps - 1)
     def _():
         def finish(j, carry):
-            out_ref[at(j), k_at:v_at] = unrope(dk_scr[at(j), :], at(j))
+            out_ref[at(j), k_at:v_at] = unrope(dk_scr[at(j), :], j)
             out_ref[at(j), v_at : v_at + HEAD_DIM] = dv_scr[at(j), :].astype(BF16)
             return carry
 
         lax.fori_loop(0, steps, finish, 0)
 
 
-def attn_bwd(qkv, grad_out, lse, cos, sin, blk):
+def attn_bwd(qkv, grad_out, lse, blk):
     seq, width = qkv.shape
     n_q = width // HEAD_DIM - 2
     return call(
@@ -397,8 +400,10 @@
             whole((seq, width)),
             pl.BlockSpec((blk, n_q * HEAD_DIM), lambda i: (i, 0)),
             pl.BlockSpec((8 * n_q, blk), lambda i: (0, i)),
-            whole((seq, HEAD_DIM)),
-            whole((seq, HEAD_DIM)),
+            whole((seq // blk, HEAD_DIM)),
+            whole((seq // blk, HEAD_DIM)),
+            whole((blk, HEAD_DIM)),
+            whole((blk, HEAD_DIM)),
         ],
         out_specs=whole((seq, width)),
         out_shape=jax.ShapeDtypeStruct((seq, width), BF16),
@@ -406,7 +411,87 @@
         + [pltpu.VMEM((seq, blk), F32)] * n_q
         + [pltpu.VMEM((seq, blk), BF16)] * n_q,
         name="attn_bwd",
-    )(qkv, grad_out, lse, cos, sin)
+    )(qkv, grad_out, lse, *rope_tables(jnp.arange(seq // blk) * blk), *rope_tables(jnp.arange(blk)))
+
+
+def outer_kernel(a_ref, b_ref, out_ref):
+    out_ref[...] = tn(a_ref[...], b_ref[...]).astype(BF16)
+
+
+def outer(a, b):
+    seq, dim = a.shape
+    width = b.shape[1]
+    tile = min(512, dim)
+    return call(
+        outer_kernel,
+        2 * seq * dim * width,
+        2 * seq * dim,
+        grid=(dim // tile,),
+        in_specs=[pl.BlockSpec((seq, tile), lambda i: (0, i)), whole((seq, width))],
+        out_specs=pl.BlockSpec((tile, width), lambda i: (i, 0)),
+        out_shape=jax.ShapeDtypeStruct((dim, width), BF16),
+        name="outer",
+    )(a, b)
+
+
+def heads_kernel(a_ref, w_ref, out_ref):
+    out_ref[0] = nt(a_ref[...], w_ref[...]).astype(BF16)
+
+
+def to_head_groups(a, w, groups):
+    tok, dim = a.shape
+    width = w.shape[0] // groups
+    return call(
+        heads_kernel,
+        2 * tok * dim * w.shape[0],
+        2 * dim * w.shape[0],
+        grid=(groups,),
+        in_specs=[whole((tok, dim)), pl.BlockSpec((width, dim), lambda j: (j, 0))],
+        out_specs=pl.BlockSpec((1, tok, width), lambda j: (j, 0, 0)),
+        out_shape=jax.ShapeDtypeStruct((groups, tok, width), BF16),
+        name="to_head_groups",
+    )(a, w)
+
+
+def from_heads_kernel(g_ref, wq_ref, wk_ref, wv_ref, out_ref, acc_ref):
+    step = pl.program_id(0)
+    qw = wq_ref.shape[1]
+    grad = g_ref[0]
+    total = nt(grad[:, :qw], wq_ref[...]) + nt(grad[:, qw:], jnp.concatenate([wk_ref[...], wv_ref[...]], axis=1))
+
+    @pl.when(step == 0)
+    def _():
+        acc_ref[...] = total
+
+    @pl.when(step > 0)
+    def _():
+        acc_ref[...] += total
+
+    @pl.when(step == pl.num_programs(0) - 1)
+    def _():
+        out_ref[...] = acc_ref[...].astype(BF16)
+
+
+def from_head_groups(grads, w_query, w_key, w_value):
+    groups, tok, width = grads.shape
+    dim = w_query.shape[0]
+    qw, kw = w_query.shape[1] // groups, w_key.shape[1] // groups
+    return call(
+        from_heads_kernel,
+        2 * tok * dim * width * groups,
+        2 * dim * width * groups,
+        grid=(groups,),
+        in_specs=[
+            pl.BlockSpec((1, tok, width), lambda j: (j, 0, 0)),
+            pl.BlockSpec((dim, qw), lambda j: (0, j)),
+            pl.BlockSpec((dim, kw), lambda j: (0, j)),
+            pl.BlockSpec((dim, kw), lambda j: (0, j)),
+        ],
+        out_specs=whole((tok, dim)),
+        out_shape=jax.ShapeDtypeStruct((tok, dim), BF16),
+        scratch_shapes=[pltpu.VMEM((tok, dim), F32)],
+        name="from_head_groups",
+    )(grads, w_query, w_key, w_value)
 
 
 def act_grads(gate, up, grad_act):
@@ -640,24 +725,23 @@
         def _():
             forward(i)
 
-        @pl.when(i >= tiles)
+        @pl.when((i >= tiles) & (i < slots))
         def _():
             weights(i - tiles)
 
         events(step * slots + i)
+
+        @pl.when(i == slots - 1)
+        def _():
+            ring.start(step)
+
         return carry
 
-    lax.fori_loop(0, slots, slot_body, 0)
-    ring.start(step)
-
-    @pl.when(step == blocks - 1)
-    def _():
-        def tail(slot, carry):
-            events(slot)
-            return carry
-
-        lax.fori_loop(blocks * slots, (blocks + 1) * slots + max(delays), tail, 0)
-
+    last = step == blocks - 1
+    lax.fori_loop(0, jnp.where(last, 2 * slots + max(delays), slots), slot_body, 0)
+
+    @pl.when(last)
+    def _():
         def drain(b, carry):
             ring.drain(b)
             return carry
@@ -822,7 +906,6 @@
         ff_local = w_gate.shape[1] // mlp_size
         rows = dim // dp_size
         attn_blk = min(512, n_seq // 2)
-        cos_all, sin_all = rope_tables(jnp.arange(n_seq))
 
         def to_heads(stacked):
             return lax.all_to_all(stacked, seq_axes, 0, 0, tiled=True)
@@ -850,23 +933,18 @@
         g_mlp, late_hidden = lax.optimization_barrier((g_mlp, grad_hidden))
         g_mlp = gather(g_mlp, ("z", "x", "y", "c"))
 
-        grad_attn = jnp.einsum("td,jed->jte", late_hidden, w_out_heads, preferred_element_type=F32).astype(BF16)
+        grad_attn = to_head_groups(late_hidden, w_out, sp_size)
         grad_attn = to_heads(grad_attn).reshape(n_seq, q_width)
-        g_out = tn(grad_hidden_y, attn_y).astype(BF16).reshape(mlp_outer, rows, q_width)
+        g_out = outer(grad_hidden_y, attn_y).reshape(mlp_outer, rows, q_width)
         g_out = ring_reduce(g_out, inv_batch, 1, "z", "x", 5)
 
-        gqkv = attn_bwd(qkv, grad_attn, lse, cos_all, sin_all, attn_blk)
+        gqkv = attn_bwd(qkv, grad_attn, lse, attn_blk)
         gqkv_tok = to_heads(gqkv.reshape(sp_size, n_local, q_width + 2 * k_width))
-        flat = lambda t: jnp.transpose(t, (1, 0, 2)).reshape(n_local, -1)
-        grad_normed = (
-            nt(flat(gqkv_tok[:, :, :q_width]), w_query)
-            + nt(flat(gqkv_tok[:, :, q_width : q_width + k_width]), w_key)
-            + nt(flat(gqkv_tok[:, :, q_width + k_width :]), w_value)
-        ).astype(BF16)
+        grad_normed = from_head_groups(gqkv_tok, w_query, w_key, w_value)
         grad_tok_norm, g_norm_attn = norm_bwd(grad_normed, unit_attn, inv_attn, norm_attn)
         grad_tokens = (grad_hidden.astype(F32) + grad_tok_norm).astype(BF16)
 
-        g_attn = tn(normed_full, gqkv).astype(BF16).reshape(dp_size, rows, q_width + 2 * k_width)
+        g_attn = outer(normed_full, gqkv).reshape(dp_size, rows, q_width + 2 * k_width)
         gains = jnp.stack([g_norm_attn.reshape(dp_size, rows), g_norm_mlp.reshape(dp_size, rows)], axis=1)
         gains = jnp.pad(gains.astype(BF16), ((0, 0), (0, rows - 2), (0, 0)))
         g_attn = ring_reduce(jnp.concatenate([g_attn, gains], axis=2), inv_batch, 2, "z", "y", 2)

time: 818 us -> 812 us (level)
  Pallas kernels: 406 us -> 443 us
  matrix products: 38.5 us -> 6.21 us
    pallas_call x0 -> x4, Pallas kernels: none -> 37 us  [the longest x2 15.5 us: outer(): call(outer_kernel, 2 * seq * dim * width, 2 * seq * dim, grid=(dim // til...]
    dot_general x6 -> x0, matrix products: 32.3 us -> none  [the longest x2 16.5 us: tn(): lax.dot_general(a, b, (((0,), (0,)), ((), ())), preferred_element_type=F32)]
  transfers between devices with their start and end apart: 8 -> 8, of which waited for: 4 -> 4; matrix products, arithmetic and copies ran while one was open for 5% -> 1% of each run, Pallas kernels for 26% -> 29%
where the time goes in v2:
time: 812 us; the launch traced here: 810 us
  Pallas kernels  443 us (55%)
  waiting for transfers between devices  302 us (37%)
  other arithmetic  20.1 us (2%)
  starting transfers between devices  18.2 us (2%)
  between operations  14.1 us (2%)
    all_gather x5, waiting for transfers between devices, gather(): return lax.all_gather(local, axes, axis=0, tiled=True)  297 us
    pallas_call x1, Pallas kernels, mlp_ring(): pl.pallas_call(functools.partial(mlp_ring_kernel, n, subs, scale, blocks,...  98.7 us
    pallas_call x2, Pallas kernels, ring_reduce(): pl.pallas_call(functools.partial(ring_reduce_kernel, n, subs, scale, slow...  73.3 us
    pallas_call x1, Pallas kernels, spread_mlp(): call(functools.partial(spread_mlp_kernel, groups, ff_local, min(256, ff_l...  71.9 us
    pallas_call x1, Pallas kernels, mlp_grad_input(): call(mlp_kernel, 5 * 2 * tok * dim * width, 3 * 2 * dim * width, grid=(wi...  43.7 us
    pallas_call x1, Pallas kernels, gather_qkv(): pl.pallas_call(gather_qkv_kernel, in_specs=[vmem, anywhere, anywhere, any...  42.1 us
    pallas_call x1, Pallas kernels, spread_attn(): call(functools.partial(spread_attn_kernel, groups, q_width, k_width), tot...  27.3 us
    pallas_call x1, Pallas kernels, attn_fwd(): pl.pallas_call(functools.partial(attn_fwd_kernel, blk, n_q), grid=(steps,...  25.4 us
  transfers between devices with their start and end apart: 8, of which 4 were waited for; matrix products, arithmetic and copies ran while one was open for 1% of the time, Pallas kernels for 29%

profile of v2, /device:TPU:6, one launch (start us, length us, event | category | flops | bytes accessed | tf_op | source)
XLA Modules:
  0.0 809.8 jit_solution(15521114857495548329)
XLA Ops:
  8.6 1.5 fusion.23
  10.2 1.3 fusion.20.x_ref
  13.0 42.1 %gather_qkv.1 = (bf16[2048,2048]{1,0:T(8,128)(2,1)}, bf16[2048,512]{1,0:T(8,128)(2,1)}) custom-call(bf16[256,2048]{1,0:T(8,128)(2,1)} %fusion.20.x_ref, bf16[2048,2048]{1,0:T(8,128)(2,1)} %wq_ref.3, bf16[2048,1024]{1,0:T(8,128)(2,1)} %wk_ref.3, bf16[2048,1024]{1,0:T(8,128)(2,1)} %wv_ref.3, f32[8,128]{1,0:T(8,128)} %get-tuple-element.58.cos_blk, ...), custom_call_target="tpu_custom_call" | custom-call | flops 20000000000 | bytes 25165824 | tf_op jit(solution)/shard_map/gather_qkv/pallas_call | solution.py:192
  55.1 25.4 %attn_fwd.1 = (bf16[2048,256]{1,0:T(8,128)(2,1)}, f32[16,2048]{1,0:T(8,128)}, bf16[8,256,256]{2,1,0:T(8,128)(2,1)}) custom-call(bf16[2048,512]{1,0:T(8,128)(2,1)} %get-tuple-element.24.qkv_ref), custom_call_target="tpu_custom_call" | custom-call | flops 4294967296 | bytes 2097152 | tf_op jit(solution)/shard_map/attn_fwd/pallas_call | solution.py:308
  80.5 6.2 fusion.18
  86.8 1.3 fusion.16.m_ref
  89.1 43.7 %mlp_grad_input.1 = bf16[256,2048]{1,0:T(8,128)(2,1)} custom-call(bf16[256,2048]{1,0:T(8,128)(2,1)} %fusion.16.m_ref, bf16[256,2048]{1,0:T(8,128)(2,1)} %bitcast.39, bf16[2048,6144]{1,0:T(8,128)(2,1)} %wg_all.1, bf16[2048,6144]{1,0:T(8,128)(2,1)} %wu_all.1, bf16[6144,2048]{1,0:T(8,128)(2,1)} %wd_all.1), custom_call_target="tpu_custom_call" | custom-call | flops 32212254720 | bytes 75497472 | tf_op jit(solution)/shard_map/mlp_grad_input/pallas_call | solution.py:528
  132.7 2.2 fusion.19
  135.0 1.7 fusion.15.a_ref
  136.7 6.4 all-to-all-start.2
  143.2 51.4 %all-gather.15.cloned.1.call-done = bf16[1,2048,2048]{2,1,0:T(8,128)(2,1)} async-done(((bf16[1,256,2048]{2,1,0:T(8,128)(2,1)}), bf16[1,2048,2048]{2,1,0:T(8,128)(2,1)}) %all-gather.15.cloned.1.call-update) | async-done | bytes 8388624 | tf_op jit(solution)/shard_map/all_gather | solution.py:914
  194.6 98.7 %mlp_ring.1 = bf16[2304,128]{1,0:T(8,128)(2,1)} custom-call(bf16[2048,2048]{1,0:T(8,128)(2,1)} %all-gather.7.cloned.1.call-done.m_all, bf16[2048,2048]{1,0:T(8,128)(2,1)} %bitcast.50, bf16[2048,6144]{1,0:T(8,128)(2,1)} %wg_all.1, bf16[2048,6144]{1,0:T(8,128)(2,1)} %wu_all.1, bf16[6144,2048]{1,0:T(8,128)(2,1)} %wd_all.1), custom_call_target="tpu_custom_call" | custom-call | flops 57982058496 | bytes 16777216 | tf_op jit(solution)/shard_map/mlp_ring/pallas_call | solution.py:759
  293.2 8.8 %to_head_groups.1 = bf16[8,256,256]{2,1,0:T(8,128)(2,1)} custom-call(bf16[256,2048]{1,0:T(8,128)(2,1)} %fusion.15.a_ref, bf16[2048,2048]{1,0:T(8,128)(2,1)} %w_ref.1), custom_call_target="tpu_custom_call" | custom-call | flops 2147483648 | bytes 8388608 | tf_op jit(solution)/shard_map/to_head_groups/pallas_call | solution.py:444
  302.0 5.9 all-to-all-start
  310.7 6.7 outer.3
  317.4 4.4 all-to-all-done
  322.7 23.8 %attn_bwd.1.b_ref = bf16[2048,512]{1,0:T(8,128)(2,1)} custom-call(bf16[2048,512]{1,0:T(8,128)(2,1)} %get-tuple-element.24.qkv_ref, bf16[2048,256]{1,0:T(8,128)(2,1)} %bitcast.44, f32[16,2048]{1,0:T(8,128)} %get-tuple-element.27.lse_ref, f32[4,128]{1,0:T(4,128)} %get-tuple-element.62.cos_blk, f32[4,128]{1,0:T(4,128)} %get-tuple-element.63.sin_blk, ...), custom_call_target="tpu_custom_call" | custom-call | flops 10737418240 | bytes 4194304 | tf_op jit(solution)/shard_map/attn_bwd/pallas_call | solution.py:394
  346.5 5.6 all-to-all-start.1
  352.2 44.4 %ring_reduce.3 = bf16[128,256]{1,0:T(8,128)(2,1)} custom-call(bf16[4,4,128,256]{3,2,1,0:T(8,128)(2,1)} %bitcast.43), custom_call_target="tpu_custom_call" | custom-call | flops 40000000000 | bytes 1048576 | tf_op jit(solution)/shard_map/ring_reduce/pallas_call | solution.py:803
  396.5 8.8 %outer.2 = bf16[2048,512]{1,0:T(8,128)(2,1)} custom-call(bf16[2048,2048]{1,0:T(8,128)(2,1)} %get-tuple-element.28.a_ref, bf16[2048,512]{1,0:T(8,128)(2,1)} %attn_bwd.1.b_ref), custom_call_target="tpu_custom_call" | custom-call | flops 4294967296 | bytes 8388608 | tf_op jit(solution)/shard_map/outer/pallas_call | solution.py:425
  405.4 1.3 copy-done.4
  406.7 12.7 %from_head_groups.1 = bf16[256,2048]{1,0:T(8,128)(2,1)} custom-call(bf16[8,256,512]{2,1,0:T(8,128)(2,1)} %copy-done.4, bf16[2048,2048]{1,0:T(8,128)(2,1)} %wq_ref.3, bf16[2048,1024]{1,0:T(8,128)(2,1)} %wk_ref.3, bf16[2048,1024]{1,0:T(8,128)(2,1)} %wv_ref.3), custom_call_target="tpu_custom_call" | custom-call | flops 4294967296 | bytes 16777216 | tf_op jit(solution)/shard_map/from_head_groups/pallas_call | solution.py:479
  419.4 2.2 fusion.22
  421.7 1.8 pad_maximum_fusion.g_ref
  423.5 28.9 %ring_reduce.2 = bf16[128,640]{1,0:T(8,128)(2,1)} custom-call(bf16[4,4,128,640]{3,2,1,0:T(8,128)(2,1)} %pad_maximum_fusion.g_ref), custom_call_target="tpu_custom_call" | custom-call | flops 40000000000 | bytes 2621440 | tf_op jit(solution)/shard_map/ring_reduce/pallas_call | solution.py:803
  452.4 1.0 slice.12
  455.4 1.7 fusion.24
  457.1 92.6 %all-gather.11.cloned.1.call-done.in_ref = bf16[17408,768]{1,0:T(8,128)(2,1)} async-done(((bf16[136,768]{1,0:T(8,128)(2,1)}), bf16[17408,768]{1,0:T(8,128)(2,1)}) %all-gather.11.cloned.1.call-update) | async-done | bytes 26738704 | tf_op jit(solution)/shard_map/all_gather | solution.py:914
  549.8 27.3 %spread_attn.1 = (f32[2048,2048]{1,0:T(8,128)}, f32[2048,1024]{1,0:T(8,128)}, f32[2048,1024]{1,0:T(8,128)}, f32[2048,2048]{1,0:T(8,128)}, f32[128,128]{1,0:T(8,128)}) custom-call(bf16[17408,768]{1,0:T(8,128)(2,1)} %all-gather.11.cloned.1.call-done.in_ref), custom_call_target="tpu_custom_call" | custom-call | flops 13369344 | bytes 80216064 | tf_op jit(solution)/shard_map/spread_attn/pallas_call | solution.py:864
  577.1 1.5 fusion.31
  578.6 152.7 %all-gather.13.cloned.1.call-done.in_ref = bf16[294912,128]{1,0:T(8,128)(2,1)} async-done(((bf16[2304,128]{1,0:T(8,128)(2,1)}), bf16[294912,128]{1,0:T(8,128)(2,1)}) %all-gather.13.cloned.1.call-update) | async-done | bytes 75497488 | tf_op jit(solution)/shard_map/all_gather | solution.py:914
  731.3 71.9 %spread_mlp.1 = (f32[2048,6144]{1,0:T(8,128)}, f32[2048,6144]{1,0:T(8,128)}, f32[6144,2048]{1,0:T(8,128)}) custom-call(bf16[294912,128]{1,0:T(8,128)(2,1)} %all-gather.13.cloned.1.call-done.in_ref), custom_call_target="tpu_custom_call" | custom-call | flops 37748736 | bytes 226492416 | tf_op jit(solution)/shard_map/spread_mlp/pallas_call | solution.py:826
  (69 shorter events, 9.8 us)
Async XLA Ops:
  7.2 3.0 copy-start.1
  7.2 136.0 %all-gather.7.cloned.1.call-start = ((), (), s32[]{:S(2)}) async-start(), calls=%async_computation.3 | async-start | bytes 9437184 | tf_op jit(solution)/shard_map/all_gather | solution.py:914
  8.6 3.7 copy-start.10
  10.2 2.8 copy-start.13
  80.5 6.2 copy-start.15
  88.1 106.5 %all-gather.15.cloned.1.call-start = ((), (), s32[]{:S(2)}) async-start(), calls=%async_computation.7 | async-start | bytes 9437184 | tf_op jit(solution)/shard_map/all_gather | solution.py:914
  88.8 221.8 %all-gather.9.cloned.1.call-start = ((), (), s32[]{:S(2)}) async-start(), calls=%async_computation.4 | async-start | bytes 9437184 | tf_op jit(solution)/shard_map/all_gather | solution.py:914
  132.7 2.2 copy-start.6
  132.7 2.2 copy-start.7
  136.7 165.3 %all-to-all-start.2 = ((bf16[8,256,256]{2,1,0:T(8,128)(2,1)}), bf16[8,256,256]{2,1,0:T(8,128)(2,1)S(1)}, u32[]{:S(2)}, u32[]{:S(2)}) async-start(bf16[8,256,256]{2,1,0:T(8,128)(2,1)} %get-tuple-element.25), calls=%async_computation.2 | async-start | bytes 2097152 | tf_op jit(solution)/shard_map/all_to_all | solution.py:930
  302.0 8.6 %copy-start.5 = (bf16[8,256,256]{2,1,0:T(8,128)(2,1)}, bf16[8,256,256]{2,1,0:T(8,128)(2,1)S(1)}, u32[]{:S(2)}) copy-start(bf16[8,256,256]{2,1,0:T(8,128)(2,1)S(1)} %all-to-all-done.2) | copy-start | bytes 3145732
  302.0 19.7 %all-to-all-start = ((bf16[8,256,256]{2,1,0:T(8,128)(2,1)}), bf16[8,256,256]{2,1,0:T(8,128)(2,1)S(1)}, u32[]{:S(2)}, u32[]{:S(2)}) async-start(bf16[8,256,256]{2,1,0:T(8,128)(2,1)} %to_head_groups.1), calls=%async_computation | async-start | bytes 2097152 | tf_op jit(solution)/shard_map/all_to_all | solution.py:911
  321.8 1.0 copy-start.9
  346.5 58.8 %all-to-all-start.1 = ((bf16[8,256,512]{2,1,0:T(8,128)(2,1)}), bf16[8,256,512]{2,1,0:T(8,128)(2,1)S(1)}, u32[]{:S(2)}, u32[]{:S(2)}) async-start(bf16[8,256,512]{2,1,0:T(8,128)(2,1)} %bitcast.42), calls=%async_computation.1 | async-start | bytes 4194304 | tf_op jit(solution)/shard_map/all_to_all | solution.py:911
  352.2 197.6 %all-gather.11.cloned.1.call-start = ((), (), s32[]{:S(2)}) async-start(), calls=%async_computation.5 | async-start | bytes 26947584 | tf_op jit(solution)/shard_map/all_gather | solution.py:914
  405.3 14.0 %copy-start.2 = (bf16[1,256,2048]{2,1,0:T(8,128)(2,1)S(1)}, bf16[1,256,2048]{2,1,0:T(8,128)(2,1)}, u32[]{:S(2)}) copy-start(bf16[1,256,2048]{2,1,0:T(8,128)(2,1)} %param.11) | copy-start | bytes 3145732
  405.3 14.0 %copy-start.11 = (f32[2048]{0:T(1024)S(1)}, f32[2048]{0:T(1024)}, u32[]{:S(2)}) copy-start(f32[2048]{0:T(1024)} %copy-done.10) | copy-start | bytes 24580
  405.3 14.0 %copy-start.14 = (f32[256]{0:T(256)S(1)}, f32[256]{0:T(256)}, u32[]{:S(2)}) copy-start(f32[256]{0:T(256)} %copy-done.13) | copy-start | bytes 3076
  405.4 1.3 copy-start.4
  419.4 2.4 copy-start.8
  423.5 30.6 %copy-start.12 = (bf16[128,256]{1,0:T(8,128)(2,1)S(1)}, bf16[128,256]{1,0:T(8,128)(2,1)}, u32[]{:S(2)}) copy-start(bf16[128,256]{1,0:T(8,128)(2,1)} %ring_reduce.3) | copy-start | bytes 196612
  423.5 31.9 %copy-start.3 = (bf16[256,2048]{1,0:T(8,128)(2,1)S(1)}, bf16[256,2048]{1,0:T(8,128)(2,1)}, u32[]{:S(2)}) copy-start(bf16[256,2048]{1,0:T(8,128)(2,1)} %from_head_groups.1) | copy-start | bytes 3145732
  452.4 3.0 copy-start
  454.8 276.5 %all-gather.13.cloned.1.call-start = ((), (), s32[]{:S(2)}) async-start(), calls=%async_computation.6 | async-start | bytes 76087296 | tf_op jit(solution)/shard_map/all_gather | solution.py:914
Sparse Core Ops, SparseCore 0:
  88.2 53.3 all-gather.6
  143.4 51.1 all-gather.14
  196.9 49.2 all-gather.8
  454.9 94.8 all-gather.10
  552.7 178.5 all-gather.12
